TPU v7x, 32 devices: a whole 2x2x4 slice. The times are simulated.
32 devices in a mesh: dp: 8 (over z, y), mp: 4 (over x, core).
Axes of the slice: x: 2, y: 2, z: 4, core: 2. Of those that a mesh axis runs over, the one named last changes fastest.
Arguments:
- image_tokens: bfloat16 [8, 192, 3072], P('dp'), may hold values from -6 to 6
- text_tokens: bfloat16 [8, 64, 3072], P('dp'), may hold values from -6 to 6
- null_prompt: bfloat16 [64, 3072], replicated, may hold values from -6 to 6
- drop_flags: int32 [8], P('dp'), may hold values 0 or 1
- time_index: int32 [8], P('dp'), may hold values from 0 to 31
- modulation: float32 [32, 3, 3072], replicated, may hold values from -3 to 3
- w_up: bfloat16 [3072, 12288], P('dp', 'mp'), may hold values from -0.109375 to 0.109375
- w_down: bfloat16 [12288, 3072], P('mp', 'dp'), may hold values from -0.0546875 to 0.0546875
- d_output: bfloat16 [8, 256, 3072], P('dp'), may hold values from -6 to 6
Outputs:
- block_out: bfloat16 [8, 256, 3072], P('dp')
- d_tokens: bfloat16 [8, 256, 3072], P('dp')
- grad_up: float32 [3072, 12288], P('dp', 'mp')
- grad_down: float32 [12288, 3072], P('mp', 'dp')
- grad_null: float32 [64, 3072], replicated
All inputs are finite; a program needn't handle non-finite values. No bound on the sum of `drop_flags` on one device may be relied on, other than what follows from the above.
Results may differ from a plain program's by a relative error of at most 0.017.
Values may be sent and summed in bfloat16 or wider, within the bound.
A program may use at most 128 MiB of HBM per device.

v0:
```python
import functools

import jax
import jax.numpy as jnp
from jax import lax
from jax.sharding import PartitionSpec as P

EPS = 1e-06
BF16 = jnp.bfloat16
F32 = jnp.float32


def gelu_tanh(values):
    return jax.nn.gelu(values, approximate=True)


def dot(left, right, dims):
    return lax.dot_general(left, right, (dims, ((), ())), preferred_element_type=F32)


def swap(values, axis, size, bit):
    return lax.ppermute(values, axis, [(i, i ^ bit) for i in range(size)])


def shards(
    dp,
    mp,
    image_tokens,
    text_tokens,
    null_prompt,
    drop_flags,
    time_index,
    modulation,
    w_up,
    w_down,
    d_output,
):
    lines = [list(range(parity, dp, 2)) for parity in range(2)]
    per_line = dp // 2
    bits = []
    bit = 1
    while bit < mp:
        bits.append(bit)
        bit *= 2

    d_rows, ff_m = w_up.shape
    f = ff_m // dp
    width = d_rows * dp

    up_own = lax.all_to_all(
        w_up.reshape(d_rows, dp, f).transpose(1, 0, 2), "dp", 0, 0, tiled=True
    ).reshape(width, f)
    down_own = (
        lax.all_to_all(w_down.reshape(dp, f, d_rows), "dp", 0, 0, tiled=True)
        .transpose(1, 0, 2)
        .reshape(f, width)
    )
    up_other = swap(up_own, "dp", dp, 1)
    down_other = swap(down_own, "dp", dp, 1)

    m = lax.axis_index("mp")
    n_text = text_tokens.shape[1] // mp
    n_image = image_tokens.shape[1] // mp
    all_text = text_tokens.shape[1]

    def share(text_part, image_part):
        t = lax.dynamic_slice_in_dim(text_part, m * n_text, n_text, 0)
        i = lax.dynamic_slice_in_dim(image_part, m * n_image, n_image, 0)
        return jnp.concatenate([t, i], axis=0)

    dropped = drop_flags[0] == 1
    joined32 = share(
        jnp.where(dropped, null_prompt, text_tokens[0]), image_tokens[0]
    ).astype(F32)
    d_out32 = share(d_output[0, :all_text], d_output[0, all_text:]).astype(F32)
    level = lax.dynamic_index_in_dim(modulation, time_index[0], 0, keepdims=False)
    shift, scale, gate = level[0][None], level[1][None], level[2][None]
    centred = joined32 - jnp.mean(joined32, axis=-1, keepdims=True)
    inv_std = lax.rsqrt(jnp.mean(centred * centred, axis=-1, keepdims=True) + EPS)
    normed = centred * inv_std
    mod_in = (normed * (1.0 + scale) + shift).astype(BF16)
    d_branch = (d_out32 * gate).astype(BF16)

    def gather(rows):
        rows = lax.all_gather(rows, "dp", axis=0, tiled=True, axis_index_groups=lines)
        for b in reversed(bits):
            rows = jnp.concatenate([rows, swap(rows, "mp", mp, b)], axis=0)
        return rows

    def scatter(own, other, block_own, block_other, contract):
        def product(rows):
            return dot(own[rows], block_own, contract) + dot(other[rows], block_other, contract)

        half = own.shape[0] // 2
        sent = swap(product(slice(half, None)).astype(BF16), "mp", mp, bits[0])
        total = product(slice(0, half)) + sent.astype(F32)
        for b in bits[1:]:
            half = total.shape[0] // 2
            total = total[:half] + swap(total[half:].astype(BF16), "mp", mp, b).astype(F32)
        parts = lax.all_to_all(
            total.astype(BF16).reshape(per_line, -1, width),
            "dp",
            0,
            0,
            tiled=True,
            axis_index_groups=lines,
        )
        return jnp.sum(parts.astype(F32), axis=0)

    tokens = gather(mod_in)
    d_tok = gather(d_branch)

    def half_block(up, down):
        pre = dot(tokens, up, ((1,), (0,)))
        hid, back = jax.vjp(gelu_tanh, pre)
        d_hid = dot(d_tok, down, ((1,), (1,)))
        return hid.astype(BF16), back(d_hid)[0].astype(BF16)

    hid_own, dpre_own = half_block(up_own, down_own)
    hid_other, dpre_other = half_block(up_other, down_other)
    branch = scatter(hid_own, hid_other, down_own, down_other, ((1,), (0,)))
    d_mod = scatter(dpre_own, dpre_other, up_own, up_other, ((1,), (1,)))

    up_sent = dot(tokens, dpre_other, ((0,), (0,))).astype(BF16)
    down_sent = dot(hid_other, d_tok, ((0,), (0,))).astype(BF16)
    up_back = swap(up_sent, "dp", dp, 1)
    down_back = swap(down_sent, "dp", dp, 1)
    g_up = dot(tokens, dpre_own, ((0,), (0,))) + up_back.astype(F32)
    g_down = dot(hid_own, d_tok, ((0,), (0,))) + down_back.astype(F32)
    grad_up = (
        lax.all_to_all(g_up.astype(BF16).reshape(dp, d_rows, f), "dp", 0, 0, tiled=True)
        .transpose(1, 0, 2)
        .reshape(d_rows, ff_m)
        .astype(F32)
    )
    grad_down = (
        lax.all_to_all(
            g_down.astype(BF16).reshape(f, dp, d_rows).transpose(1, 0, 2),
            "dp",
            0,
            0,
            tiled=True,
        )
        .reshape(ff_m, d_rows)
        .astype(F32)
    )

    block_out = (joined32 + gate * branch).astype(BF16)
    d_normed = d_mod * (1.0 + scale)
    d_full = d_out32 + inv_std * (
        d_normed
        - jnp.mean(d_normed, axis=-1, keepdims=True)
        - normed * jnp.mean(d_normed * normed, axis=-1, keepdims=True)
    )
    null_part = jnp.where(dropped, d_full[:n_text], F32(0.0)).astype(BF16)
    null_sum = lax.psum(null_part, "dp")

    def whole(rows):
        every = lax.all_gather(rows, "mp", axis=0)
        return jnp.concatenate(
            [
                every[:, :n_text].reshape(-1, width),
                every[:, n_text:].reshape(-1, width),
            ],
            axis=0,
        )[None]

    grad_null = lax.all_gather(null_sum, "mp", axis=0, tiled=True).astype(F32)
    return (whole(block_out), whole(d_full.astype(BF16)), grad_up, grad_down, grad_null)


def solution(mesh):
    placed = (
        P("dp", None, None),
        P("dp", None, None),
        P(),
        P("dp"),
        P("dp"),
        P(),
        P("dp", "mp"),
        P("mp", "dp"),
        P("dp", None, None),
    )
    return jax.shard_map(
        functools.partial(shards, mesh.shape["dp"], mesh.shape["mp"]),
        mesh=mesh,
        in_specs=placed,
        out_specs=(P("dp", None, None), P("dp", None, None), P("dp", "mp"), P("mp", "dp"), P()),
        check_vma=False,
    )
```

profile of v0, /device:TPU:9, one launch (start us, length us, event | category | flops | bytes accessed | tf_op | source)
XLA Modules:
  0.0 626.0 jit_solution(12918581351889117631)
XLA Ops:
  13.5 5.7 all-to-all-start.1
  21.2 53.8 %all-gather.5.cloned.1.call-done = bf16[256,3072]{1,0:T(8,128)(2,1)} async-done(((bf16[64,3072]{1,0:T(8,128)(2,1)}), bf16[256,3072]{1,0:T(8,128)(2,1)}) %all-gather.5.cloned.1.call-update) | async-done | bytes 1572880 | tf_op jit(solution)/shard_map/all_gather | solution.py:85
  76.4 48.5 %all-gather.9.cloned.1.call-done = bf16[256,3072]{1,0:T(8,128)(2,1)} async-done(((bf16[64,3072]{1,0:T(8,128)(2,1)}), bf16[256,3072]{1,0:T(8,128)(2,1)}) %all-gather.9.cloned.1.call-update) | async-done | bytes 1572880 | tf_op jit(solution)/shard_map/all_gather | solution.py:85
  142.9 17.1 %collective-permute-done.6 = bf16[256,3072]{1,0:T(8,128)(2,1)} collective-permute-done((bf16[256,3072]{1,0:T(8,128)(2,1)}, bf16[256,3072]{1,0:T(8,128)(2,1)}, u32[]{:S(2)}, u32[]{:S(2)}) %collective-permute-start.6) | collective-permute-done | bytes 1572896 | tf_op jit(solution)/shard_map/ppermute | solution.py:22
  178.9 9.9 %all-to-all-done = bf16[8,384,384]{1,2,0:T(8,128)(2,1)} async-done(((bf16[8,384,384]{1,2,0:T(8,128)(2,1)}), bf16[8,384,384]{1,2,0:T(8,128)(2,1)}, u32[]{:S(2)}, u32[]{:S(2)}) %all-to-all-start) | async-done | bytes 2359328 | tf_op jit(solution)/shard_map/all_to_all | solution.py:50
  207.0 21.7 %collective-permute-done.3 = bf16[384,3072]{0,1:T(8,128)(2,1)} collective-permute-done((bf16[384,3072]{0,1:T(8,128)(2,1)S(1)}, bf16[384,3072]{0,1:T(8,128)(2,1)}, u32[]{:S(2)}, u32[]{:S(2)}) %collective-permute-start.3) | collective-permute-done | bytes 2359328 | tf_op jit(solution)/shard_map/ppermute | solution.py:22
  228.7 6.2 fusion.47
  239.3 39.8 %collective-permute-done.2 = bf16[3072,384]{1,0:T(8,128)(2,1)S(1)} collective-permute-done((bf16[3072,384]{1,0:T(8,128)(2,1)}, bf16[3072,384]{1,0:T(8,128)(2,1)S(1)}, u32[]{:S(2)}, u32[]{:S(2)}) %collective-permute-start.2) | collective-permute-done | bytes 2359328 | tf_op jit(solution)/shard_map/ppermute | solution.py:22
  309.4 30.3 %collective-permute-done.10 = bf16[3072,384]{1,0:T(8,128)(2,1)S(1)} collective-permute-done((bf16[3072,384]{1,0:T(8,128)(2,1)S(1)}, bf16[3072,384]{1,0:T(8,128)(2,1)S(1)}, u32[]{:S(2)}, u32[]{:S(2)}) %collective-permute-start.10) | collective-permute-done | bytes 2359328 | tf_op jit(solution)/shard_map/ppermute | solution.py:22
  350.0 6.3 %fusion.30 = f32[512,3072]{1,0:T(8,128)} fusion(bf16[3072,384]{1,0:T(8,128)(2,1)} %copy-done.2, bf16[1024,384]{1,0:T(8,128)(2,1)S(1)} %copy-done.15), kind=kOutput, calls=%fused_computation.66 | convolution fusion | flops 1207959552 | bytes 9043968 | tf_op jit(solution)/shard_map/dot_general | solution.py:18
  356.3 8.1 %convert_add_fusion = f32[512,3072]{1,0:T(8,128)} fusion(bf16[512,3072]{1,0:T(8,128)(2,1)} %collective-permute-done.8, f32[512,3072]{1,0:T(8,128)S(1)} %bitcast.86, f32[512,3072]{1,0:T(8,128)} %fusion.30), kind=kLoop, calls=%fused_computation | loop fusion | flops 4718592 | bytes 22020096 | tf_op jit(solution)/shard_map/add | solution.py:96
  372.7 6.8 %convert_add_fusion.1 = f32[512,3072]{1,0:T(8,128)} fusion(bf16[512,3072]{1,0:T(8,128)(2,1)} %collective-permute-done.4, f32[512,3072]{1,0:T(8,128)S(1)} %bitcast.84, f32[512,3072]{1,0:T(8,128)S(1)} %fusion.37), kind=kLoop, calls=%fused_computation.2 | loop fusion | flops 4718592 | bytes 22020096 | tf_op jit(solution)/shard_map/add | solution.py:96
  383.2 18.7 %collective-permute-done.9 = bf16[256,3072]{1,0:T(8,128)(2,1)} collective-permute-done((bf16[256,3072]{1,0:T(8,128)(2,1)}, bf16[256,3072]{1,0:T(8,128)(2,1)}, u32[]{:S(2)}, u32[]{:S(2)}) %collective-permute-start.9) | collective-permute-done | bytes 1572896 | tf_op jit(solution)/shard_map/ppermute | solution.py:22
  410.5 7.2 %convolution_convert_fusion = bf16[384,3072]{1,0:T(8,128)(2,1)} fusion(bf16[1024,384]{1,0:T(8,128)(2,1)} %copy-done.13, bf16[1024,3072]{1,0:T(8,128)(2,1)} %constant_dynamic-update-slice_fusion.3), kind=kOutput, calls=%fused_computation.7 | convolution fusion | flops 2417098752 | bytes 9437184 | tf_op jit(solution)/shard_map/dot_general | solution.py:18
  420.8 14.8 %collective-permute-done.5 = bf16[256,3072]{1,0:T(8,128)(2,1)} collective-permute-done((bf16[256,3072]{1,0:T(8,128)(2,1)}, bf16[256,3072]{1,0:T(8,128)(2,1)}, u32[]{:S(2)}, u32[]{:S(2)}) %collective-permute-start.5) | collective-permute-done | bytes 1572896 | tf_op jit(solution)/shard_map/ppermute | solution.py:22
  440.8 8.6 %all-to-all-start.2 = ((bf16[4,64,3072]{2,1,0:T(8,128)(2,1)}), bf16[4,64,3072]{2,1,0:T(8,128)(2,1)S(1)}, u32[]{:S(2)}, u32[]{:S(2)}) async-start(bf16[4,64,3072]{2,1,0:T(8,128)(2,1)} %bitcast.105), calls=%async_computation.2 | async-start | bytes 3145728 | tf_op jit(solution)/shard_map/all_to_all | solution.py:100
  449.6 14.9 %collective-permute-done.11 = bf16[384,3072]{1,0:T(8,128)(2,1)} collective-permute-done((bf16[384,3072]{1,0:T(8,128)(2,1)}, bf16[384,3072]{1,0:T(8,128)(2,1)}, u32[]{:S(2)}, u32[]{:S(2)}) %collective-permute-start.11) | collective-permute-done | bytes 2359328 | tf_op jit(solution)/shard_map/ppermute | solution.py:22
  464.5 6.1 add_convert_fusion.2
  481.8 8.7 %all-to-all-start.5 = ((bf16[8,384,384]{2,1,0:T(8,128)(2,1)}), bf16[8,384,384]{2,1,0:T(8,128)(2,1)S(1)}, u32[]{:S(2)}, u32[]{:S(2)}) async-start(bf16[8,384,384]{2,1,0:T(8,128)(2,1)} %bitcast.101), calls=%async_computation.5 | async-start | bytes 4718592 | tf_op jit(solution)/shard_map/all_to_all | solution.py:137
  499.1 44.5 %all-to-all-done.5 = bf16[8,384,384]{2,1,0:T(8,128)(2,1)S(1)} async-done(((bf16[8,384,384]{2,1,0:T(8,128)(2,1)}), bf16[8,384,384]{2,1,0:T(8,128)(2,1)S(1)}, u32[]{:S(2)}, u32[]{:S(2)}) %all-to-all-start.5) | async-done | bytes 2359328 | tf_op jit(solution)/shard_map/all_to_all | solution.py:137
  546.3 24.6 %all-reduce.2.cloned.1.call-done = bf16[16,3072]{1,0:T(8,128)(2,1)} async-done(((bf16[16,3072]{1,0:T(8,128)(2,1)}), bf16[16,3072]{1,0:T(8,128)(2,1)}) %all-reduce.2.cloned.1.call-update) | async-done | bytes 98320 | tf_op jit(solution)/shard_map/psum | solution.py:156
  570.9 9.2 %all_gather.21 = bf16[64,3072]{1,0:T(8,128)(2,1)S(1)} all-gather(bf16[16,3072]{1,0:T(8,128)(2,1)} %all-reduce.2.cloned.1.call-done), channel_id=1, replica_groups=mesh['dp'=8,'mp'=4] {'mp'}, dimensions={0}, use_global_device_ids=true | all-gather | bytes 491520 | tf_op jit(solution)/shard_map/all_gather | solution.py:168
  581.1 13.7 %all-gather.7.cloned.1.call-done = bf16[4,64,3072]{2,1,0:T(8,128)(2,1)} async-done(((bf16[1,64,3072]{2,1,0:T(8,128)(2,1)}), bf16[4,64,3072]{2,1,0:T(8,128)(2,1)}) %all-gather.7.cloned.1.call-update) | async-done | bytes 1572880 | tf_op jit(solution)/shard_map/all_gather | solution.py:159
  597.4 19.0 %all-gather.11.cloned.1.call-done = bf16[4,64,3072]{2,1,0:T(8,128)(2,1)} async-done(((bf16[1,64,3072]{2,1,0:T(8,128)(2,1)}), bf16[4,64,3072]{2,1,0:T(8,128)(2,1)}) %all-gather.11.cloned.1.call-update) | async-done | bytes 1572880 | tf_op jit(solution)/shard_map/all_gather | solution.py:159
  (166 shorter events, 165.6 us)
Async XLA Ops:
  7.2 67.8 %all-gather.5.cloned.1.call-start = ((), (), s32[]{:S(2)}) async-start(), calls=%async_computation.6 | async-start | bytes 1966080 | tf_op jit(solution)/shard_map/all_gather | solution.py:85
  13.5 116.8 %all-to-all-start.1 = ((bf16[8,384,384]{2,1,0:T(8,128)(2,1)}), bf16[8,384,384]{2,1,0:T(8,128)(2,1)S(1)}, u32[]{:S(2)}, u32[]{:S(2)}) async-start(bf16[8,384,384]{2,1,0:T(8,128)(2,1)} %bitcast.115), calls=%async_computation.1 | async-start | bytes 4718592 | tf_op jit(solution)/shard_map/all_to_all | solution.py:54
  19.3 105.6 %all-gather.9.cloned.1.call-start = ((), (), s32[]{:S(2)}) async-start(), calls=%async_computation.8 | async-start | bytes 1966080 | tf_op jit(solution)/shard_map/all_gather | solution.py:85
  20.3 110.1 %copy-start.12 = (bf16[1,64,3072]{2,1,0:T(8,128)(2,1)}, bf16[1,64,3072]{2,1,0:T(8,128)(2,1)S(1)}, u32[]{:S(2)}) copy-start(bf16[1,64,3072]{2,1,0:T(8,128)(2,1)S(1)} %slice.82) | copy-start | bytes 1179652
  75.0 61.9 %collective-permute-start = (bf16[256,3072]{1,0:T(8,128)(2,1)}, bf16[256,3072]{1,0:T(8,128)(2,1)}, u32[]{:S(2)}, u32[]{:S(2)}) collective-permute-start(bf16[256,3072]{1,0:T(8,128)(2,1)} %all-gather.5.cloned.1.call-done), channel_id=1, source_target_pairs={{0,2},{1,3},{2,0},{3,1},{4,6},{5,7},{6,4},{7,5},{8,10},{9,11},{10,... | collective-permute-start | bytes 4718600 | tf_op jit(solution)/shard_map/ppermute | solution.py:22
  124.9 35.1 %collective-permute-start.6 = (bf16[256,3072]{1,0:T(8,128)(2,1)}, bf16[256,3072]{1,0:T(8,128)(2,1)}, u32[]{:S(2)}, u32[]{:S(2)}) collective-permute-start(bf16[256,3072]{1,0:T(8,128)(2,1)} %all-gather.9.cloned.1.call-done), channel_id=1, source_target_pairs={{0,2},{1,3},{2,0},{3,1},{4,6},{5,7},{6,4},{7,5},{8,10},{9,11},{10,... | collective-permute-start | bytes 4718600 | tf_op jit(solution)/shard_map/ppermute | solution.py:22
  131.9 57.0 %all-to-all-start = ((bf16[8,384,384]{1,2,0:T(8,128)(2,1)}), bf16[8,384,384]{1,2,0:T(8,128)(2,1)}, u32[]{:S(2)}, u32[]{:S(2)}) async-start(bf16[8,384,384]{1,2,0:T(8,128)(2,1)} %bitcast.103), calls=%async_computation | async-start | bytes 4718592 | tf_op jit(solution)/shard_map/all_to_all | solution.py:50
  140.7 53.0 %collective-permute-start.1 = (bf16[512,3072]{1,0:T(8,128)(2,1)}, bf16[512,3072]{1,0:T(8,128)(2,1)}, u32[]{:S(2)}, u32[]{:S(2)}) collective-permute-start(bf16[512,3072]{1,0:T(8,128)(2,1)} %pad_maximum_fusion), channel_id=1, source_target_pairs={{0,1},{1,0},{2,3},{3,2},{4,5},{5,4},{6,7},{7,6},{8,9},{9,8},{10,11... | collective-permute-start | bytes 9437192 | tf_op jit(solution)/shard_map/ppermute | solution.py:22
  163.3 34.2 %collective-permute-start.7 = (bf16[512,3072]{1,0:T(8,128)(2,1)}, bf16[512,3072]{1,0:T(8,128)(2,1)}, u32[]{:S(2)}, u32[]{:S(2)}) collective-permute-start(bf16[512,3072]{1,0:T(8,128)(2,1)} %pad_maximum_fusion.1), channel_id=1, source_target_pairs={{0,1},{1,0},{2,3},{3,2},{4,5},{5,4},{6,7},{7,6},{8,9},{9,8},{10,11... | collective-permute-start | bytes 9437192 | tf_op jit(solution)/shard_map/ppermute | solution.py:22
  169.6 59.1 %collective-permute-start.3 = (bf16[384,3072]{0,1:T(8,128)(2,1)S(1)}, bf16[384,3072]{0,1:T(8,128)(2,1)}, u32[]{:S(2)}, u32[]{:S(2)}) collective-permute-start(bf16[384,3072]{0,1:T(8,128)(2,1)S(1)} %bitcast.87), channel_id=1, source_target_pairs={{0,4},{4,0},{8,12},{12,8},{16,20},{20,16},{24,28},{28,24},{1,5},{5... | collective-permute-start | bytes 7077896 | tf_op jit(solution)/shard_map/ppermute | solution.py:22
  193.1 86.0 %collective-permute-start.2 = (bf16[3072,384]{1,0:T(8,128)(2,1)}, bf16[3072,384]{1,0:T(8,128)(2,1)S(1)}, u32[]{:S(2)}, u32[]{:S(2)}) collective-permute-start(bf16[3072,384]{1,0:T(8,128)(2,1)} %bitcast.91), channel_id=1, source_target_pairs={{0,4},{4,0},{8,12},{12,8},{16,20},{20,16},{24,28},{28,24},{1,5},{5... | collective-permute-start | bytes 7077896 | tf_op jit(solution)/shard_map/ppermute | solution.py:22
  287.4 52.2 %collective-permute-start.10 = (bf16[3072,384]{1,0:T(8,128)(2,1)S(1)}, bf16[3072,384]{1,0:T(8,128)(2,1)S(1)}, u32[]{:S(2)}, u32[]{:S(2)}) collective-permute-start(bf16[3072,384]{1,0:T(8,128)(2,1)S(1)} %convolution_convert_fusion.1), channel_id=1, source_target_pairs={{0,4},{4,0},{8,12},{12,8},{16,20},{20,16},{24,28},{28,24},{1,5},{5... | collective-permute-start | bytes 7077896 | tf_op jit(solution)/shard_map/ppermute | solution.py:22
  292.9 63.4 %collective-permute-start.8 = (bf16[512,3072]{1,0:T(8,128)(2,1)}, bf16[512,3072]{1,0:T(8,128)(2,1)}, u32[]{:S(2)}, u32[]{:S(2)}) collective-permute-start(bf16[512,3072]{1,0:T(8,128)(2,1)} %add_convert_fusion), channel_id=1, source_target_pairs={{0,1},{1,0},{2,3},{3,2},{4,5},{5,4},{6,7},{7,6},{8,9},{9,8},{10,11... | collective-permute-start | bytes 9437192 | tf_op jit(solution)/shard_map/ppermute | solution.py:22
  300.5 72.2 %collective-permute-start.4 = (bf16[512,3072]{1,0:T(8,128)(2,1)}, bf16[512,3072]{1,0:T(8,128)(2,1)}, u32[]{:S(2)}, u32[]{:S(2)}) collective-permute-start(bf16[512,3072]{1,0:T(8,128)(2,1)} %add_convert_fusion.1), channel_id=1, source_target_pairs={{0,1},{1,0},{2,3},{3,2},{4,5},{5,4},{6,7},{7,6},{8,9},{9,8},{10,11... | collective-permute-start | bytes 9437192 | tf_op jit(solution)/shard_map/ppermute | solution.py:22
  344.5 61.3 %all-to-all-start.4 = ((bf16[8,384,384]{2,1,0:T(8,128)(2,1)}), bf16[8,384,384]{2,1,0:T(8,128)(2,1)}, u32[]{:S(2)}, u32[]{:S(2)}) async-start(bf16[8,384,384]{2,1,0:T(8,128)(2,1)} %bitcast.116), calls=%async_computation.4 | async-start | bytes 4718592 | tf_op jit(solution)/shard_map/all_to_all | solution.py:131
  367.9 34.0 %collective-permute-start.9 = (bf16[256,3072]{1,0:T(8,128)(2,1)}, bf16[256,3072]{1,0:T(8,128)(2,1)}, u32[]{:S(2)}, u32[]{:S(2)}) collective-permute-start(bf16[256,3072]{1,0:T(8,128)(2,1)} %slice.154), channel_id=1, source_target_pairs={{0,2},{1,3},{2,0},{3,1},{4,6},{5,7},{6,4},{7,5},{8,10},{9,11},{10,... | collective-permute-start | bytes 4718600 | tf_op jit(solution)/shard_map/ppermute | solution.py:22
  382.8 52.8 %collective-permute-start.5 = (bf16[256,3072]{1,0:T(8,128)(2,1)}, bf16[256,3072]{1,0:T(8,128)(2,1)}, u32[]{:S(2)}, u32[]{:S(2)}) collective-permute-start(bf16[256,3072]{1,0:T(8,128)(2,1)} %slice.155), channel_id=1, source_target_pairs={{0,2},{1,3},{2,0},{3,1},{4,6},{5,7},{6,4},{7,5},{8,10},{9,11},{10,... | collective-permute-start | bytes 4718600 | tf_op jit(solution)/shard_map/ppermute | solution.py:22
  405.8 35.0 %all-to-all-start.3 = ((bf16[4,64,3072]{2,1,0:T(8,128)(2,1)}), bf16[4,64,3072]{2,1,0:T(8,128)(2,1)}, u32[]{:S(2)}, u32[]{:S(2)}) async-start(bf16[4,64,3072]{2,1,0:T(8,128)(2,1)} %bitcast.106), calls=%async_computation.3 | async-start | bytes 3145728 | tf_op jit(solution)/shard_map/all_to_all | solution.py:100
  417.7 46.8 %collective-permute-start.11 = (bf16[384,3072]{1,0:T(8,128)(2,1)}, bf16[384,3072]{1,0:T(8,128)(2,1)}, u32[]{:S(2)}, u32[]{:S(2)}) collective-permute-start(bf16[384,3072]{1,0:T(8,128)(2,1)} %convolution_convert_fusion), channel_id=1, source_target_pairs={{0,4},{4,0},{8,12},{12,8},{16,20},{20,16},{24,28},{28,24},{1,5},{5... | collective-permute-start | bytes 7077896 | tf_op jit(solution)/shard_map/ppermute | solution.py:22
  440.8 39.9 %all-to-all-start.2 = ((bf16[4,64,3072]{2,1,0:T(8,128)(2,1)}), bf16[4,64,3072]{2,1,0:T(8,128)(2,1)S(1)}, u32[]{:S(2)}, u32[]{:S(2)}) async-start(bf16[4,64,3072]{2,1,0:T(8,128)(2,1)} %bitcast.105), calls=%async_computation.2 | async-start | bytes 3145728 | tf_op jit(solution)/shard_map/all_to_all | solution.py:100
  449.3 121.6 %all-reduce.2.cloned.1.call-start = ((), (), s32[]{:S(2)}) async-start(), calls=%async_computation.10 | async-start | bytes 196608 | tf_op jit(solution)/shard_map/psum | solution.py:156
  481.8 61.7 %all-to-all-start.5 = ((bf16[8,384,384]{2,1,0:T(8,128)(2,1)}), bf16[8,384,384]{2,1,0:T(8,128)(2,1)S(1)}, u32[]{:S(2)}, u32[]{:S(2)}) async-start(bf16[8,384,384]{2,1,0:T(8,128)(2,1)} %bitcast.101), calls=%async_computation.5 | async-start | bytes 4718592 | tf_op jit(solution)/shard_map/all_to_all | solution.py:137
  490.5 104.2 %all-gather.7.cloned.1.call-start = ((), (), s32[]{:S(2)}) async-start(), calls=%async_computation.7 | async-start | bytes 1966080 | tf_op jit(solution)/shard_map/all_gather | solution.py:159
  493.7 122.7 %all-gather.11.cloned.1.call-start = ((), (), s32[]{:S(2)}) async-start(), calls=%async_computation.9 | async-start | bytes 1966080 | tf_op jit(solution)/shard_map/all_gather | solution.py:159
  (36 other events, 409.0 us)
Sparse Core Ops, SparseCore 0:
  13.6 61.3 all-gather.4
  77.1 47.6 all-gather.8
  477.2 93.6 all-reduce.1
  572.9 21.7 all-gather.6
  596.7 19.6 all-gather.10
where the time goes:
time: 638 us; the launch traced here: 626 us
  waiting for transfers between devices  378 us (59%)
  matrix products  73.8 us (12%)
  starting transfers between devices  50.5 us (8%)
  other arithmetic  49.7 us (8%)
  local copies, waits for them, and re-layouts  49 us (8%)
  between operations  16.1 us (3%)
  blocking collectives  9.2 us (1%)
    ppermute x12, waiting for transfers between devices, swap(): return lax.ppermute(values, axis, [(i, i ^ bit) for i in range(size)])  157 us
    all_gather x2, waiting for transfers between devices, gather(): lax.all_gather(rows, 'dp', axis=0, tiled=True, axis_index_groups=lines)  102 us
    dot_general x16, matrix products, dot(): lax.dot_general(left, right, (dims, ((), ())), preferred_element_type=F32)  73.8 us
    all_to_all x1, waiting for transfers between devices, shards(): lax.all_to_all(g_down.astype(BF16).reshape(f, dp, d_rows).transpose(1, 0,...  44.5 us
    all_gather x2, waiting for transfers between devices, whole(): every = lax.all_gather(rows, 'mp', axis=0)  32.7 us
    psum x1, waiting for transfers between devices, shards(): null_sum = lax.psum(null_part, 'dp')  24.6 us
    unnamed x69, local copies, waits for them, and re-layouts  17.3 us
    add x2, other arithmetic, scatter(): total = product(slice(0, half)) + sent.astype(F32)  14.9 us
  transfers between devices with their start and end apart: 23, of which 16 were waited for; matrix products, arithmetic and copies ran while one was open for 24% of the time, Pallas kernels for 0%

commit v1 on v0

--- a/solution.py
+++ b/solution.py
@@ -3,11 +3,16 @@
 import jax
 import jax.numpy as jnp
 from jax import lax
+from jax.experimental import pallas as pl
+from jax.experimental.pallas import tpu as pltpu
 from jax.sharding import PartitionSpec as P
 
 EPS = 1e-06
 BF16 = jnp.bfloat16
 F32 = jnp.float32
+MESH = pl.DeviceIdType.MESH
+Y = 2
+C = 2
 
 
 def gelu_tanh(values):
@@ -22,7 +27,7 @@
     return lax.ppermute(values, axis, [(i, i ^ bit) for i in range(size)])
 
 
-def shards(
+def generic(
     dp,
     mp,
     image_tokens,
@@ -169,6 +174,695 @@
     return (whole(block_out), whole(d_full.astype(BF16)), grad_up, grad_down, grad_null)
 
 
+class Place:
+    def __init__(self, dp, mp):
+        self.Z, self.X = dp // Y, mp // C
+        d, m = lax.axis_index("dp"), lax.axis_index("mp")
+        self.z, self.y = d // Y, d % Y
+        self.x, self.c = m // C, m % C
+        self.d, self.m = d, m
+
+    def at_z(self, z):
+        return (z * Y + self.y, self.m)
+
+    def at_y(self):
+        return (self.z * Y + 1 - self.y, self.m)
+
+    def at_x(self, x):
+        return (self.d, x * C + self.c)
+
+    def at_c(self):
+        return (self.d, self.x * C + 1 - self.c)
+
+    def z_plus(self, j):
+        return lax.rem(self.z + j, self.Z)
+
+    def x_plus(self, j):
+        return lax.rem(self.x + j, self.X)
+
+    def meet(self):
+        barrier = pltpu.get_barrier_semaphore()
+        peers = [self.at_z(self.z_plus(j)) for j in range(1, self.Z)]
+        peers += [self.at_x(self.x_plus(j)) for j in range(1, self.X)]
+        peers += [self.at_y(), self.at_c()]
+        for peer in peers:
+            pl.semaphore_signal(barrier, inc=1, device_id=peer, device_id_type=MESH)
+        pl.semaphore_wait(barrier, len(peers))
+
+
+class Copies:
+    def __init__(self, sems):
+        self.sems, self.used, self.open = sems, 0, []
+
+    def go(self, src, dst, recv, device, when=None):
+        sem = self.sems.at[self.used]
+        self.used += 1
+
+        source, target, peer = src(), dst(), device()
+
+        def make():
+            return pltpu.make_async_remote_copy(
+                src_ref=source,
+                dst_ref=target,
+                send_sem=sem,
+                recv_sem=recv,
+                device_id=peer,
+                device_id_type=MESH,
+            )
+
+        def start():
+            make().start()
+
+        def finish():
+            make().wait_send()
+
+        guard(when, start)
+        self.open.append((when, finish))
+
+    def local(self, src, dst, when=None):
+        sem = self.sems.at[self.used]
+        self.used += 1
+
+        source, target = src(), dst()
+
+        def make():
+            return pltpu.make_async_copy(source, target, sem)
+
+        def start():
+            make().start()
+
+        def finish():
+            make().wait()
+
+        guard(when, start)
+        self.open.append((when, finish))
+
+    def finish(self):
+        for when, wait in self.open:
+            guard(when, wait)
+        self.open = []
+
+
+def guard(when, act):
+    if when is None:
+        act()
+    else:
+        pl.when(when)(act)
+
+
+def landed(place, ref, recv, when=None):
+    def act():
+        pltpu.make_async_remote_copy(
+            src_ref=ref(),
+            dst_ref=ref(),
+            send_sem=recv,
+            recv_sem=recv,
+            device_id=place.at_y(),
+            device_id_type=MESH,
+        ).wait_recv()
+
+    guard(when, act)
+
+
+def tile(index, size):
+    return pl.ds(pl.multiple_of(index * size, size), size)
+
+
+def arrive(dp, mp, nch, own, w_up, w_down, tok, up, down, send, z_tok, x_tok, c_tok, z_w, y_w):
+    p = Place(dp, mp)
+    Z, X = p.Z, p.X
+    dr = w_up.shape[0]
+    fz = w_up.shape[1] // Z
+    fch = fz // nch
+    p.meet()
+    cp = Copies(send)
+
+    def up_src(z, k):
+        return w_up.at[:, pl.ds(pl.multiple_of(z * fz + k * fch, fch), fch)]
+
+    def down_src(z, k):
+        return w_down.at[pl.ds(pl.multiple_of(z * fz + k * fch, fch), fch), :]
+
+    def up_dst(d, k):
+        return up.at[tile(d, dr), pl.ds(k * fch, fch)]
+
+    def down_dst(d, k):
+        return down.at[pl.ds(k * fch, fch), tile(d, dr)]
+
+    kinds = ((up_src, up_dst), (down_src, down_dst))
+
+    slots = [(0, p.z, None)]
+    for s in range(Z - 1):
+        slots.append((1 + 2 * s, p.z - 1 - s, p.z - 1 - s >= 0))
+        slots.append((2 + 2 * s, p.z + 1 + s, p.z + 1 + s < Z))
+
+    def block(sample, quarter):
+        return tok.at[:, sample, quarter]
+
+    def spread(slot, sample, when):
+        source = (lambda: own.at[...]) if slot == 0 else (lambda: block(sample, p.m))
+        for j in range(1, X):
+            cp.go(source, lambda: block(sample, p.m), x_tok.at[j - 1, slot], lambda j=j: p.at_x(p.x_plus(j)), when)
+        cp.go(source, lambda: block(sample, p.m), c_tok.at[0, slot], p.at_c, when)
+
+    def pass_on(s):
+        for way in (1, -1):
+            sample = p.z - s * way
+            inside = (sample >= 0) & (p.z + 1 < Z) if way == 1 else (sample < Z) & (p.z >= 1)
+            source = (lambda: own.at[...]) if s == 0 else (lambda sample=sample: block(sample, p.m))
+            cp.go(
+                source,
+                lambda sample=sample: block(sample, p.m),
+                z_tok.at[(0 if way == 1 else 1), s],
+                lambda way=way: p.at_z(p.z + way),
+                inside,
+            )
+
+    def z_weights(k):
+        for j in (2, 1, 3) if Z == 4 else range(1, Z):
+            for kind, (src, dst) in enumerate(kinds):
+                cp.go(
+                    lambda: src(p.z_plus(j), k),
+                    lambda: dst(p.d, k),
+                    z_w.at[j - 1, k, kind],
+                    lambda: p.at_z(p.z_plus(j)),
+                )
+
+    pass_on(0)
+    spread(*slots[0])
+    for k in range(nch):
+        for kind, (src, dst) in enumerate(kinds):
+            cp.go(lambda: src(p.z, k), lambda: dst(p.d, k), y_w.at[0, k, kind], p.at_y)
+    z_weights(0)
+    cp.local(lambda: own.at[...], lambda: block(p.z, p.m))
+    for k in range(nch):
+        for src, dst in kinds:
+            cp.local(lambda: src(p.z, k), lambda: dst(p.d, k))
+
+    for s in range(Z - 1):
+        for side in (0, 1):
+            slot, sample, valid = slots[1 + 2 * s + side]
+            landed(p, lambda: block(sample, p.m), z_tok.at[side, s], valid)
+        if s < Z - 2:
+            pass_on(s + 1)
+        for side in (0, 1):
+            spread(*slots[1 + 2 * s + side])
+    for k in range(1, nch):
+        z_weights(k)
+
+    def forward(k):
+        for j in (2, 1, 3) if Z == 4 else range(1, Z):
+            d_src = lax.rem(p.z - j + Z, Z) * Y + p.y
+            for kind, (_, dst) in enumerate(kinds):
+                landed(p, lambda: dst(d_src, k), z_w.at[j - 1, k, kind])
+                cp.go(lambda: dst(d_src, k), lambda: dst(d_src, k), y_w.at[j, k, kind], p.at_y)
+
+    forward(0)
+    for slot, sample, valid in slots:
+        for j in range(1, X):
+            quarter = lax.rem(p.x - j + X, X) * C + p.c
+            landed(p, lambda: block(sample, quarter), x_tok.at[j - 1, slot], valid)
+            cp.go(lambda: block(sample, quarter), lambda: block(sample, quarter), c_tok.at[j, slot], p.at_c, valid)
+    for k in range(1, nch):
+        forward(k)
+    for slot, sample, valid in slots:
+        for j in range(X):
+            quarter = lax.rem(p.x - j + X, X) * C + 1 - p.c
+            landed(p, lambda: block(sample, quarter), c_tok.at[j, slot], valid)
+    for k in range(nch):
+        for j in range(Z):
+            d_src = lax.rem(p.z - j + Z, Z) * Y + 1 - p.y
+            for kind, (_, dst) in enumerate(kinds):
+                landed(p, lambda: dst(d_src, k), y_w.at[j, k, kind])
+    cp.finish()
+
+
+def add_into(target, other, rows, step):
+    def body(i, _):
+        at = pl.ds(pl.multiple_of(i * step, step), step)
+        target[at, :] = (target[at, :].astype(F32) + other[at, :].astype(F32)).astype(BF16)
+        return 0
+
+    lax.fori_loop(0, rows // step, body, 0)
+
+
+def depart(
+    dp,
+    mp,
+    nch,
+    n_text,
+    g_up,
+    g_down,
+    branch,
+    d_mod,
+    joined,
+    d_out,
+    levels,
+    drop,
+    fin_all,
+    null_all,
+    up_out,
+    down_out,
+    y_up,
+    y_down,
+    c_buf,
+    x_buf,
+    r_buf,
+    l_buf,
+    fin,
+    null,
+    null_y,
+    null_z,
+    send,
+    y_g,
+    z_g,
+    c_s,
+    x_s,
+    r_s,
+    l_s,
+    f_x,
+    f_c,
+    n_y,
+    n_z,
+    n_x,
+    n_c,
+):
+    p = Place(dp, mp)
+    Z, X = p.Z, p.X
+    fz = g_up.shape[1]
+    fch = fz // nch
+    width = g_up.shape[0]
+    dr = width // (Z * Y)
+    n = joined.shape[0]
+    p.meet()
+    cp = Copies(send)
+    partial = (branch, d_mod)
+    order = []
+    for i in range((Z + 1) // 2):
+        order += [Z - 1 - i] + ([i] if i != Z - 1 - i else [])
+
+    def rows_of(sample, x, c):
+        return pl.ds(pl.multiple_of(sample * (X * C * n) + (x * C + c) * n, n), n)
+
+    for t in order:
+        for i in range(2):
+            for j in range(X):
+                x = p.x_plus(j + 1)
+                cp.go(
+                    lambda: partial[i].at[rows_of(t, x, 1 - p.c), :],
+                    lambda: c_buf.at[i, t, x],
+                    c_s.at[i, t, j],
+                    p.at_c,
+                )
+
+    def up_rows(z, y):
+        return tile(z * Y + y, dr)
+
+    jorder = [2, 1, 3, 0] if Z == 4 else [j for j in range(1, Z)] + [0]
+    pieces = [(k, j, kind) for k in range(nch) for j in jorder for kind in range(2)]
+
+    def g_ref(ref, kind, z, y, k):
+        cols = pl.ds(k * fch, fch)
+        return ref.at[up_rows(z, y), cols] if kind == 0 else ref.at[cols, up_rows(z, y)]
+
+    def y_ref(kind, z, k):
+        cols = pl.ds(k * fch, fch)
+        return y_up.at[tile(z, dr), cols] if kind == 0 else y_down.at[cols, tile(z, dr)]
+
+    def out_ref(kind, z, k):
+        cols = pl.ds(pl.multiple_of(z * fz + k * fch, fch), fch)
+        return up_out.at[:, cols] if kind == 0 else down_out.at[cols, :]
+
+    for k, j, kind in pieces:
+        z = p.z_plus(j)
+        cp.go(
+            lambda: g_ref((g_up, g_down)[kind], kind, z, 1 - p.y, k),
+            lambda: y_ref(kind, z, k),
+            y_g.at[j, k, kind],
+            p.at_y,
+        )
+
+    def gradient(k, j, kind):
+        z = p.z_plus(j)
+        landed(p, lambda: y_ref(kind, z, k), y_g.at[j, k, kind])
+        add_into(y_ref(kind, z, k), g_ref((g_up, g_down)[kind], kind, z, p.y, k), dr if kind == 0 else fch, 64)
+        if j == 0:
+            cp.local(lambda: y_ref(kind, z, k), lambda: out_ref(kind, p.z, k))
+        else:
+            cp.go(
+                lambda: y_ref(kind, z, k),
+                lambda: out_ref(kind, p.z, k),
+                z_g.at[j - 1, k, kind],
+                lambda: p.at_z(z),
+            )
+
+    def core_stage(t, i):
+        for j in range(X):
+            x = p.x_plus(j + 1)
+            landed(p, lambda: c_buf.at[i, t, x], c_s.at[i, t, j])
+            add_into(c_buf.at[i, t, x], partial[i].at[rows_of(t, x, p.c), :], n, 16)
+            if j < X - 1:
+                cp.go(
+                    lambda: c_buf.at[i, t, x],
+                    lambda: x_buf.at[j, i, t],
+                    x_s.at[j, i, t],
+                    lambda: p.at_x(x),
+                )
+
+    def x_stage(t, i):
+        for j in range(X - 1):
+            landed(p, lambda: x_buf.at[j, i, t], x_s.at[j, i, t])
+            add_into(c_buf.at[i, t, p.x], x_buf.at[j, i, t], n, 16)
+
+    def chain(t, i, hop):
+        if hop < t:
+            here = p.z == hop
+            if hop == 0:
+                cp.go(
+                    lambda: c_buf.at[i, t, p.x],
+                    lambda: r_buf.at[i, t],
+                    r_s.at[i, t],
+                    lambda: p.at_z(p.z + 1),
+                    here,
+                )
+            else:
+                landed(p, lambda: r_buf.at[i, t], r_s.at[i, t], here)
+                pl.when(here)(lambda: add_into(r_buf.at[i, t], c_buf.at[i, t, p.x], n, 16))
+                cp.go(
+                    lambda: r_buf.at[i, t],
+                    lambda: r_buf.at[i, t],
+                    r_s.at[i, t],
+                    lambda: p.at_z(p.z + 1),
+                    here,
+                )
+        low = Z - 1 - hop
+        if low > t:
+            here = p.z == low
+            if hop == 0:
+                cp.go(
+                    lambda: c_buf.at[i, t, p.x],
+                    lambda: l_buf.at[i, t],
+                    l_s.at[i, t],
+                    lambda: p.at_z(p.z - 1),
+                    here,
+                )
+            else:
+                landed(p, lambda: l_buf.at[i, t], l_s.at[i, t], here)
+                pl.when(here)(lambda: add_into(l_buf.at[i, t], c_buf.at[i, t, p.x], n, 16))
+                cp.go(
+                    lambda: l_buf.at[i, t],
+                    lambda: l_buf.at[i, t],
+                    l_s.at[i, t],
+                    lambda: p.at_z(p.z - 1),
+                    here,
+                )
+
+    sums = [(t, i) for t in order for i in range(2)]
+    pieces_left = list(pieces)
+
+    def some_gradients(count):
+        for _ in range(count):
+            if pieces_left:
+                gradient(*pieces_left.pop(0))
+
+    for item in sums:
+        core_stage(*item)
+    lag = 2
+    steps = len(sums) + lag * (Z - 2)
+    per_step = 2
+    for step in range(steps):
+        some_gradients(per_step)
+        if step < len(sums):
+            x_stage(*sums[step])
+        for hop in range(Z - 1):
+            at = step - hop * lag
+            if 0 <= at < len(sums):
+                chain(*sums[at], hop)
+
+    for i in range(2):
+        for t in range(Z):
+            here = p.z == t
+            if t > 0:
+                landed(p, lambda: r_buf.at[i, t], r_s.at[i, t], here)
+            if t < Z - 1:
+                landed(p, lambda: l_buf.at[i, t], l_s.at[i, t], here)
+
+    def total(i, at):
+        own = c_buf[i, p.z, p.x, at, :].astype(F32)
+        right = r_buf[i, p.z, at, :].astype(F32)
+        left = l_buf[i, p.z, at, :].astype(F32)
+        right = right * (p.z > 0).astype(F32)
+        left = left * (p.z < Z - 1).astype(F32)
+        return own + right + left
+
+    scale = 1.0 + levels[1:2, :]
+    gate = levels[2:3, :]
+
+    def last(b, _):
+        at = pl.ds(pl.multiple_of(b * n_text, n_text), n_text)
+        tokens = joined[at, :].astype(F32)
+        back = d_out[at, :].astype(F32)
+        centred = tokens - jnp.mean(tokens, axis=-1, keepdims=True)
+        inv_std = lax.rsqrt(jnp.mean(centred * centred, axis=-1, keepdims=True) + EPS)
+        normed = centred * inv_std
+        fin[0, at, :] = (tokens + gate * total(0, at)).astype(BF16)
+        d_normed = total(1, at) * scale
+        d_full = back + inv_std * (
+            d_normed
+            - jnp.mean(d_normed, axis=-1, keepdims=True)
+            - normed * jnp.mean(d_normed * normed, axis=-1, keepdims=True)
+        )
+        fin[1, at, :] = d_full.astype(BF16)
+
+        @pl.when(b == 0)
+        def _():
+            null[0] = (d_full * drop[0:1, :]).astype(BF16)
+
+        return 0
+
+    lax.fori_loop(0, n // n_text, last, 0)
+
+    def share(src, out, x_sem, c_sem):
+        for j in range(1, X):
+            cp.go(src, lambda: out(p.m), x_sem.at[j - 1], lambda j=j: p.at_x(p.x_plus(j)))
+        cp.go(src, lambda: out(p.m), c_sem.at[0], p.at_c)
+        cp.local(src, lambda: out(p.m))
+
+    def relay(out, x_sem, c_sem):
+        for j in range(1, X):
+            quarter = lax.rem(p.x - j + X, X) * C + p.c
+            landed(p, lambda: out(quarter), x_sem.at[j - 1])
+            cp.go(lambda: out(quarter), lambda: out(quarter), c_sem.at[j], p.at_c)
+
+    def settle(out, c_sem):
+        for j in range(X):
+            quarter = lax.rem(p.x - j + X, X) * C + 1 - p.c
+            landed(p, lambda: out(quarter), c_sem.at[j])
+
+    def fin_out(quarter):
+        return fin_all.at[:, quarter]
+
+    def null_out(quarter):
+        return null_all.at[quarter]
+
+    cp.go(lambda: null.at[0], lambda: null_y.at[...], n_y.at[0], p.at_y)
+    share(lambda: fin.at[...], fin_out, f_x, f_c)
+    some_gradients(2)
+    landed(p, lambda: null_y.at[...], n_y.at[0])
+    null[1] = (null[0].astype(F32) + null_y[...].astype(F32)).astype(BF16)
+    for j in range(1, Z):
+        cp.go(lambda: null.at[1], lambda: null_z.at[j - 1], n_z.at[j - 1], lambda: p.at_z(p.z_plus(j)))
+    some_gradients(len(pieces))
+    for j in range(1, Z):
+        landed(p, lambda: null_z.at[j - 1], n_z.at[j - 1])
+    whole_null = null[1].astype(F32)
+    for j in range(1, Z):
+        whole_null = whole_null + null_z[j - 1].astype(F32)
+    null[2] = whole_null.astype(BF16)
+    share(lambda: null.at[2], null_out, n_x, n_c)
+    relay(fin_out, f_x, f_c)
+    relay(null_out, n_x, n_c)
+    settle(fin_out, f_c)
+    settle(null_out, n_c)
+    for k, j, kind in pieces:
+        if j > 0:
+            z = lax.rem(p.z - j + Z, Z)
+            landed(p, lambda: out_ref(kind, z, k), z_g.at[j - 1, k, kind])
+    cp.finish()
+
+
+def shards(
+    dp,
+    mp,
+    image_tokens,
+    text_tokens,
+    null_prompt,
+    drop_flags,
+    time_index,
+    modulation,
+    w_up,
+    w_down,
+    d_output,
+):
+    Z, X = dp // Y, mp // C
+    d_rows, ff_m = w_up.shape
+    fz = ff_m // Z
+    nch = fz // 256
+    width = d_rows * dp
+    all_text = text_tokens.shape[1]
+    n_text = all_text // mp
+    n_image = image_tokens.shape[1] // mp
+    n = n_text + n_image
+    m = lax.axis_index("mp")
+
+    def share(text_part, image_part):
+        t = lax.dynamic_slice_in_dim(text_part, m * n_text, n_text, 0)
+        i = lax.dynamic_slice_in_dim(image_part, m * n_image, n_image, 0)
+        return jnp.concatenate([t, i], axis=0)
+
+    dropped = drop_flags[0] == 1
+    joined = share(jnp.where(dropped, null_prompt, text_tokens[0]), image_tokens[0])
+    d_out = share(d_output[0, :all_text], d_output[0, all_text:])
+    level = lax.dynamic_index_in_dim(modulation, time_index[0], 0, keepdims=False)
+    joined32 = joined.astype(F32)
+    shift, scale, gate = level[0][None], level[1][None], level[2][None]
+    centred = joined32 - jnp.mean(joined32, axis=-1, keepdims=True)
+    inv_std = lax.rsqrt(jnp.mean(centred * centred, axis=-1, keepdims=True) + EPS)
+    mod_in = (centred * inv_std * (1.0 + scale) + shift).astype(BF16)
+    d_branch = (d_out.astype(F32) * gate).astype(BF16)
+    own = jnp.stack([mod_in, d_branch])
+
+    anywhere = pl.BlockSpec(memory_space=pl.ANY)
+    vmem = pl.BlockSpec(memory_space=pltpu.VMEM)
+    dma = pltpu.SemaphoreType.DMA
+    slots = 1 + 2 * (Z - 1)
+    sends = (
+        slots * X
+        + 2 * (Z - 1)
+        + 4 * nch * Z
+        + 2 * nch
+        + 1
+        + slots * X
+    )
+    tok, up, down = pl.pallas_call(
+        functools.partial(arrive, dp, mp, nch),
+        out_shape=(
+            jax.ShapeDtypeStruct((2, Z, mp, n, width), BF16),
+            jax.ShapeDtypeStruct((width, fz), BF16),
+            jax.ShapeDtypeStruct((fz, width), BF16),
+        ),
+        in_specs=[anywhere] * 3,
+        out_specs=(anywhere,) * 3,
+        scratch_shapes=[
+            dma((sends,)),
+            dma((2, Z - 1)),
+            dma((max(X - 1, 1), slots)),
+            dma((X, slots)),
+            dma((Z - 1, nch, 2)),
+            dma((Z, nch, 2)),
+        ],
+        compiler_params=pltpu.CompilerParams(collective_id=0, has_side_effects=True),
+    )(own, w_up, w_down)
+
+    rows = Z * mp * n
+    tokens = tok[0].reshape(rows, width)
+    d_tok = tok[1].reshape(rows, width)
+    pre = dot(tokens, up, ((1,), (0,)))
+    hid, back = jax.vjp(gelu_tanh, pre)
+    d_hid = dot(d_tok, down, ((1,), (1,)))
+    hid = hid.astype(BF16)
+    d_pre = back(d_hid)[0].astype(BF16)
+    branch = dot(hid, down, ((1,), (0,))).astype(BF16)
+    d_mod = dot(d_pre, up, ((1,), (1,))).astype(BF16)
+    g_up = dot(tokens, d_pre, ((0,), (0,))).astype(BF16)
+    g_down = dot(hid, d_tok, ((0,), (0,))).astype(BF16)
+
+    drop = jnp.where(dropped, jnp.ones((8, width), F32), jnp.zeros((8, width), F32))
+    sends = (
+        2 * Z * X
+        + 4 * nch * Z
+        + 2 * Z * (X - 1)
+        + 4 * Z * (Z - 1)
+        + 1
+        + (Z - 1)
+        + 2 * (X + 1)
+        + 2 * (X - 1)
+    )
+    fin_all, null_all, up_out, down_out = pl.pallas_call(
+        functools.partial(depart, dp, mp, nch, n_text),
+        out_shape=(
+            jax.ShapeDtypeStruct((2, mp, n, width), BF16),
+            jax.ShapeDtypeStruct((mp, n_text, width), BF16),
+            jax.ShapeDtypeStruct((d_rows, ff_m), BF16),
+            jax.ShapeDtypeStruct((ff_m, d_rows), BF16),
+        ),
+        in_specs=[vmem] * 8,
+        out_specs=(anywhere,) * 4,
+        scratch_shapes=[
+            pltpu.VMEM((Z * d_rows, fz), BF16),
+            pltpu.VMEM((fz, Z * d_rows), BF16),
+            pltpu.VMEM((2, Z, X, n, width), BF16),
+            pltpu.VMEM((X - 1, 2, Z, n, width), BF16),
+            pltpu.VMEM((2, Z, n, width), BF16),
+            pltpu.VMEM((2, Z, n, width), BF16),
+            pltpu.VMEM((2, n, width), BF16),
+            pltpu.VMEM((3, n_text, width), BF16),
+            pltpu.VMEM((n_text, width), BF16),
+            pltpu.VMEM((Z - 1, n_text, width), BF16),
+            dma((sends,)),
+            dma((Z, nch, 2)),
+            dma((Z - 1, nch, 2)),
+            dma((2, Z, X)),
+            dma((X - 1, 2, Z)),
+            dma((2, Z)),
+            dma((2, Z)),
+            dma((X - 1,)),
+            dma((X,)),
+            dma((1,)),
+            dma((Z - 1,)),
+            dma((X - 1,)),
+            dma((X,)),
+        ],
+        compiler_params=pltpu.CompilerParams(
+            collective_id=1, has_side_effects=True, vmem_limit_bytes=62 * 1024 * 1024
+        ),
+    )(g_up, g_down, branch, d_mod, joined, d_out, level, drop)
+
+    def whole(every):
+        text = every[:, :n_text].reshape(-1, width)
+        image = every[:, n_text:].reshape(-1, width)
+        return jnp.concatenate([text, image], axis=0)[None]
+
+    return (
+        whole(fin_all[0]),
+        whole(fin_all[1]),
+        up_out.astype(F32),
+        down_out.astype(F32),
+        null_all.reshape(-1, width).astype(F32),
+    )
+
+
+def fits(dp, mp, image_tokens, text_tokens, w_up):
+    d_rows, ff_m = w_up.shape
+    return (
+        dp % Y == 0
+        and dp // Y > 1
+        and mp % C == 0
+        and mp // C > 1
+        and d_rows % 128 == 0
+        and ff_m % (dp // Y * 256) == 0
+        and text_tokens.shape[1] % (mp * 16) == 0
+        and image_tokens.shape[1] % text_tokens.shape[1] == 0
+    )
+
+
+def program(dp, mp, image_tokens, text_tokens, null_prompt, drop_flags, time_index, modulation, w_up, w_down, d_output):
+    path = shards if fits(dp, mp, image_tokens, text_tokens, w_up) else generic
+    return path(
+        dp, mp, image_tokens, text_tokens, null_prompt, drop_flags, time_index, modulation, w_up, w_down, d_output
+    )
+
+
 def solution(mesh):
     placed = (
         P("dp", None, None),
@@ -182,7 +876,7 @@
         P("dp", None, None),
     )
     return jax.shard_map(
-        functools.partial(shards, mesh.shape["dp"], mesh.shape["mp"]),
+        functools.partial(program, mesh.shape["dp"], mesh.shape["mp"]),
         mesh=mesh,
         in_specs=placed,
         out_specs=(P("dp", None, None), P("dp", None, None), P("dp", "mp"), P("mp", "dp"), P()),

time: 638 us -> 436 us (0.68); the launches traced: 626 us -> 436 us
  waiting for transfers between devices: 378 us -> 0 us
  Pallas kernels: 0 us -> 367 us
  starting transfers between devices: 50.5 us -> 0 us
  other arithmetic: 49.7 us -> 13.9 us
  local copies, waits for them, and re-layouts: 49 us -> 13.3 us
  matrix products: 73.8 us -> 40 us
  between operations: 16.1 us -> 2.23 us
  blocking collectives: 9.2 us -> 0 us
    pallas_call x0 -> x2, Pallas kernels: none -> 367 us  [the longest x1 201 us: shards(): pl.pallas_call(functools.partial(depart, dp, mp, nch, n_text), out_shape=...]
    ppermute x12 -> x0, waiting for transfers between devices: 157 us -> none  [swap(): return lax.ppermute(values, axis, [(i, i ^ bit) for i in range(size)])]
    all_gather x4 -> x0, waiting for transfers between devices: 135 us -> none  [the longest x2 102 us: gather(): lax.all_gather(rows, 'dp', axis=0, tiled=True, axis_index_groups=lines)]
    all_to_all x6 -> x0, waiting for transfers between devices: 60.1 us -> none  [the longest x1 44.5 us: shards(): lax.all_to_all(g_down.astype(BF16).reshape(f, dp, d_rows).transpose(1, 0,...]
    all_to_all x6 -> x0, starting transfers between devices: 38.2 us -> none  [the longest x2 13.3 us: scatter(): lax.all_to_all(total.astype(BF16).reshape(per_line, -1, width), 'dp', 0,...]
    dot_general x16 -> x6, matrix products: 73.8 us -> 40 us  [dot(): lax.dot_general(left, right, (dims, ((), ())), preferred_element_type=F32)]
    psum x1 -> x0, waiting for transfers between devices: 24.6 us -> none  [shards(): null_sum = lax.psum(null_part, 'dp')]
    unnamed x69 -> x13, local copies, waits for them, and re-layouts: 17.3 us -> 0.7 us
  transfers between devices with their start and end apart: 23 -> 0, of which waited for: 16 -> 0; matrix products, arithmetic and copies ran while one was open for 24% -> 0% of each run, Pallas kernels for 0% -> 0%
where the time goes in v1:
time: 436 us
  Pallas kernels  367 us (84%)
  matrix products  40 us (9%)
  other arithmetic  13.9 us (3%)
  local copies, waits for them, and re-layouts  13.3 us (3%)
    pallas_call x1, Pallas kernels, shards(): pl.pallas_call(functools.partial(depart, dp, mp, nch, n_text), out_shape=...  201 us
    pallas_call x1, Pallas kernels, shards(): pl.pallas_call(functools.partial(arrive, dp, mp, nch), out_shape=(jax.Sha...  166 us
    dot_general x6, matrix products, dot(): lax.dot_general(left, right, (dims, ((), ())), preferred_element_type=F32)  40 us

profile of v1, /device:TPU:9, one launch (start us, length us, event | category | flops | bytes accessed | tf_op | source)
XLA Modules:
  0.0 436.0 jit_solution(6332551968868049858)
XLA Ops:
  2.0 1.0 dynamic-slice_add_fusion
  3.1 1.0 constant_dynamic-slice_fusion.4
  4.7 1.0 dynamic-slice_select_fusion
  5.7 0.6 select_n.34.drop
  6.3 1.0 slice.44
  7.4 1.0 constant_dynamic-slice_fusion.2
  9.0 0.8 pad_maximum_fusion.2.d_out
  9.9 0.9 pad_maximum_fusion.own
  10.9 0.8 pad_maximum_fusion.1.joined
  11.7 165.8 %shard_map.128 = (bf16[2,4,4,64,3072]{4,3,2,1,0:T(8,128)(2,1)}, bf16[3072,768]{1,0:T(8,128)(2,1)}, bf16[768,3072]{1,0:T(8,128)(2,1)}) custom-call(bf16[2,64,3072]{2,1,0:T(8,128)(2,1)} %pad_maximum_fusion.own, bf16[384,3072]{1,0:T(8,128)(2,1)} %w_up.1, bf16[3072,384]{1,0:T(8,128)(2,1)} %w_down.1), custom_call_target="tpu_custom_call" | custom-call | tf_op jit(solution)/shard_map/pallas_call | solution.py:747
  177.5 6.6 %fusion.9 = (bf16[1,4,4,64,3072]{4,3,2,1,0:T(8,128)(2,1)S(1)}, bf16[1,4,4,64,3072]{4,3,2,1,0:T(8,128)(2,1)S(1)}) fusion(bf16[2,4,4,64,3072]{4,3,2,1,0:T(8,128)(2,1)} %get-tuple-element.12), kind=kLoop, calls=%fused_computation.39 | loop fusion | bytes 25165824 | tf_op jit(solution)/shard_map/slice | solution.py:769
  184.1 5.1 %fusion.10 = f32[1024,768]{1,0:T(8,128)S(1)} fusion(bf16[1024,3072]{1,0:T(8,128)(2,1)S(1)} %bitcast.49, bf16[768,3072]{1,0:T(8,128)(2,1)S(1)} %copy-done.3), kind=kOutput, calls=%fused_computation.40 | convolution fusion | flops 4831838208 | bytes 14155776 | tf_op jit(solution)/shard_map/dot_general | solution.py:23
  189.2 6.5 %fusion.6 = (bf16[1024,768]{1,0:T(8,128)(2,1)S(1)}, f32[1024,768]{1,0:T(8,128)S(1)}) fusion(f32[1024,768]{1,0:T(8,128)S(1)} %fusion.10, bf16[1024,3072]{1,0:T(8,128)(2,1)S(1)} %bitcast.47, bf16[3072,768]{1,0:T(8,128)(2,1)S(1)} %bitcast.63), kind=kOutput, calls=%fused_computation.12 | convolution fusion | flops 4847566848 | bytes 18874368 | tf_op jit(solution)/shard_map/dot_general | solution.py:23
  195.7 7.2 %convolution_convert_fusion.2.g_down = bf16[768,3072]{1,0:T(8,128)(2,1)} fusion(bf16[1024,3072]{1,0:T(8,128)(2,1)S(1)} %bitcast.50, f32[1024,768]{1,0:T(8,128)S(1)} %get-tuple-element.27), kind=kOutput, calls=%fused_computation.2 | convolution fusion | flops 4841275392 | bytes 14155776 | tf_op jit(solution)/shard_map/dot_general | solution.py:23
  202.9 6.9 %convolution_convert_fusion.3.g_up = bf16[3072,768]{1,0:T(8,128)(2,1)} fusion(bf16[1024,3072]{1,0:T(8,128)(2,1)S(1)} %bitcast.48, bf16[1024,768]{1,0:T(8,128)(2,1)S(1)} %get-tuple-element.26), kind=kOutput, calls=%fused_computation.3 | convolution fusion | flops 4834197504 | bytes 12582912 | tf_op jit(solution)/shard_map/dot_general | solution.py:23
  209.9 7.0 %convolution_convert_fusion.d_mod = bf16[1024,3072]{1,0:T(8,128)(2,1)} fusion(bf16[1024,768]{1,0:T(8,128)(2,1)S(1)} %get-tuple-element.26, bf16[3072,768]{1,0:T(8,128)(2,1)S(1)} %bitcast.63), kind=kOutput, calls=%fused_computation | convolution fusion | flops 4834983936 | bytes 12582912 | tf_op jit(solution)/shard_map/dot_general | solution.py:23
  216.9 7.2 %convolution_convert_fusion.1.branch = bf16[1024,3072]{1,0:T(8,128)(2,1)} fusion(bf16[768,3072]{1,0:T(8,128)(2,1)S(1)} %copy-done.3, f32[1024,768]{1,0:T(8,128)S(1)} %get-tuple-element.27), kind=kOutput, calls=%fused_computation.1 | convolution fusion | flops 4842061824 | bytes 14155776 | tf_op jit(solution)/shard_map/dot_general | solution.py:23
  224.1 200.7 %shard_map.129 = (bf16[2,4,64,3072]{3,2,1,0:T(8,128)(2,1)}, bf16[4,16,3072]{2,1,0:T(8,128)(2,1)}, bf16[384,3072]{1,0:T(8,128)(2,1)}, bf16[3072,384]{1,0:T(8,128)(2,1)}) custom-call(bf16[3072,768]{1,0:T(8,128)(2,1)} %convolution_convert_fusion.3.g_up, bf16[768,3072]{1,0:T(8,128)(2,1)} %convolution_convert_fusion.2.g_down, ...), custom_call_target="tpu_custom_call" | custom-call | tf_op jit(solution)/shard_map/pallas_call | solution.py:791
  424.9 2.1 slice_bitcast_fusion
  427.1 1.2 maximum_bitcast_fusion.1
  428.4 1.2 maximum_bitcast_fusion
  429.7 1.0 bitcast_convert_fusion
  430.7 2.8 convert_element_type.83
  433.5 2.5 convert_element_type.84
  (28 shorter events, 1.7 us)
Async XLA Ops:
  0.6 6.8 %slice-start = ((bf16[1,256,3072]{2,1,0:T(8,128)(2,1)}), bf16[1,192,3072]{2,1,0:T(8,128)(2,1)S(1)}, s32[]{:S(2)}) async-start(bf16[1,256,3072]{2,1,0:T(8,128)(2,1)} %param.17), calls=%async_computation | async-start | bytes 2359296 | tf_op jit(solution)/shard_map/slice | solution.py:725
  177.5 6.6 %copy-start.3 = (bf16[768,3072]{1,0:T(8,128)(2,1)S(1)}, bf16[768,3072]{1,0:T(8,128)(2,1)}, u32[]{:S(2)}) copy-start(bf16[768,3072]{1,0:T(8,128)(2,1)} %get-tuple-element.13) | copy-start | bytes 14155780
  177.5 11.7 %slice-start.1 = ((s8[4718592]{0:T(1024)(128)(4,1)}), s8[4194304]{0:T(1024)(128)(4,1)S(1)}, s32[]{:S(2)}) async-start(s8[4718592]{0:T(1024)(128)(4,1)} %bitcast.62), calls=%async_computation.1 | async-start | bytes 8388608
  184.1 5.1 %slice-start.2 = ((s8[4718592]{0:T(1024)(128)(4,1)}), s8[524288]{0:T(1024)(128)(4,1)S(1)}, s32[]{:S(2)}) async-start(s8[4718592]{0:T(1024)(128)(4,1)} %bitcast.62), calls=%async_computation.2 | async-start | bytes 1048576
  428.3 1.4 copy-start.2
  428.4 2.3 copy-start.1
  430.7 2.8 copy-start

commit v2 on v0

--- a/solution.py
+++ b/solution.py
@@ -3,11 +3,16 @@
 import jax
 import jax.numpy as jnp
 from jax import lax
+from jax.experimental import pallas as pl
+from jax.experimental.pallas import tpu as pltpu
 from jax.sharding import PartitionSpec as P
 
 EPS = 1e-06
 BF16 = jnp.bfloat16
 F32 = jnp.float32
+MESH = pl.DeviceIdType.MESH
+Y = 2
+C = 2
 
 
 def gelu_tanh(values):
@@ -22,7 +27,7 @@
     return lax.ppermute(values, axis, [(i, i ^ bit) for i in range(size)])
 
 
-def shards(
+def generic(
     dp,
     mp,
     image_tokens,
@@ -169,6 +174,810 @@
     return (whole(block_out), whole(d_full.astype(BF16)), grad_up, grad_down, grad_null)
 
 
+class Place:
+    def __init__(self, dp, mp):
+        self.Z, self.X = dp // Y, mp // C
+        d, m = lax.axis_index("dp"), lax.axis_index("mp")
+        self.z, self.y = d // Y, d % Y
+        self.x, self.c = m // C, m % C
+        self.d, self.m = d, m
+
+    def at_z(self, z):
+        return (z * Y + self.y, self.m)
+
+    def at_y(self):
+        return (self.z * Y + 1 - self.y, self.m)
+
+    def at_x(self, x):
+        return (self.d, x * C + self.c)
+
+    def at_c(self):
+        return (self.d, self.x * C + 1 - self.c)
+
+    def z_plus(self, j):
+        return lax.rem(self.z + j, self.Z)
+
+    def x_plus(self, j):
+        return lax.rem(self.x + j, self.X)
+
+    def meet(self):
+        barrier = pltpu.get_barrier_semaphore()
+        peers = [self.at_z(self.z_plus(j)) for j in range(1, self.Z)]
+        peers += [self.at_x(self.x_plus(j)) for j in range(1, self.X)]
+        peers += [self.at_y(), self.at_c()]
+        for peer in peers:
+            pl.semaphore_signal(barrier, inc=1, device_id=peer, device_id_type=MESH)
+        pl.semaphore_wait(barrier, len(peers))
+
+
+class Copies:
+    def __init__(self, sems):
+        self.sems, self.used, self.open = sems, 0, []
+
+    def go(self, src, dst, recv, device, when=None):
+        sem = self.sems.at[self.used]
+        self.used += 1
+
+        source, target, peer = src(), dst(), device()
+
+        def make():
+            return pltpu.make_async_remote_copy(
+                src_ref=source,
+                dst_ref=target,
+                send_sem=sem,
+                recv_sem=recv,
+                device_id=peer,
+                device_id_type=MESH,
+            )
+
+        def start():
+            make().start()
+
+        def finish():
+            make().wait_send()
+
+        guard(when, start)
+        self.open.append((when, finish))
+
+    def local(self, src, dst, when=None):
+        sem = self.sems.at[self.used]
+        self.used += 1
+
+        source, target = src(), dst()
+
+        def make():
+            return pltpu.make_async_copy(source, target, sem)
+
+        def start():
+            make().start()
+
+        def finish():
+            make().wait()
+
+        guard(when, start)
+        self.open.append((when, finish))
+
+    def finish(self):
+        for when, wait in self.open:
+            guard(when, wait)
+        self.open = []
+
+
+def guard(when, act):
+    if when is None:
+        act()
+    else:
+        pl.when(when)(act)
+
+
+def landed(place, ref, recv, when=None):
+    def act():
+        pltpu.make_async_remote_copy(
+            src_ref=ref(),
+            dst_ref=ref(),
+            send_sem=recv,
+            recv_sem=recv,
+            device_id=place.at_y(),
+            device_id_type=MESH,
+        ).wait_recv()
+
+    guard(when, act)
+
+
+def tile(index, size):
+    return pl.ds(pl.multiple_of(index * size, size), size)
+
+
+def add_into(target, other, rows, step):
+    def body(i, _):
+        at = pl.ds(pl.multiple_of(i * step, step), step)
+        target[at, :] = (target[at, :].astype(F32) + other[at, :].astype(F32)).astype(BF16)
+        return 0
+
+    lax.fori_loop(0, rows // step, body, 0)
+
+
+def each(first, last, act):
+    def body(i, _):
+        act(i)
+        return 0
+
+    lax.fori_loop(first, last, body, 0)
+
+
+def block_kernel(
+    dp,
+    mp,
+    nch,
+    drop,
+    level,
+    image,
+    text,
+    null_prompt,
+    d_output,
+    w_up,
+    w_down,
+    out_all,
+    d_tok_all,
+    null_all,
+    up_out,
+    down_out,
+    joined,
+    text_v,
+    null_v,
+    d_out,
+    tok,
+    up,
+    down,
+    hid,
+    d_pre,
+    g_up,
+    g_down,
+    y_up,
+    y_down,
+    s_buf,
+    c_buf,
+    x_buf,
+    l_buf,
+    fin,
+    null,
+    null_y,
+    null_z,
+    send,
+    z_tok,
+    x_tok,
+    c_tok,
+    z_w,
+    y_w,
+    y_out,
+    y_g,
+    z_out,
+    z_g,
+    c_s,
+    x_s,
+    r_s,
+    l_s,
+    f_x,
+    f_c,
+    n_y,
+    n_z,
+    n_x,
+    n_c,
+    loads,
+):
+    p = Place(dp, mp)
+    Z, X = p.Z, p.X
+    dr = w_up.shape[0]
+    fz = w_up.shape[1] // Z
+    fch = fz // nch
+    width = dr * dp
+    n_text, n_image = text.shape[1] // mp, image.shape[1] // mp
+    n = n_text + n_image
+    half = Z * X * n
+    rows = C * half
+    cp = Copies(send)
+    far = [2, 1, 3] if Z == 4 else list(range(1, Z))
+
+    def at_rows(c, z, x):
+        return pl.ds(pl.multiple_of(((c * Z + z) * X + x) * n, n), n)
+
+    every_text = text.shape[1]
+    text_at = pl.ds(pl.multiple_of(p.m * n_text, n_text), n_text)
+    image_at = pl.ds(pl.multiple_of(p.m * n_image, n_text), n_image)
+    later = pl.ds(pl.multiple_of(every_text + p.m * n_image, n_text), n_image)
+    first = [
+        pltpu.make_async_copy(text.at[0, text_at], text_v, loads.at[0]),
+        pltpu.make_async_copy(null_prompt.at[text_at], null_v, loads.at[1]),
+        pltpu.make_async_copy(image.at[0, image_at], joined.at[pl.ds(n_text, n_image)], loads.at[2]),
+        pltpu.make_async_copy(d_output.at[0, text_at], d_out.at[pl.ds(0, n_text)], loads.at[3]),
+        pltpu.make_async_copy(d_output.at[0, later], d_out.at[pl.ds(n_text, n_image)], loads.at[4]),
+    ]
+    for copy in first:
+        copy.start()
+    p.meet()
+
+    def up_src(z, k):
+        return w_up.at[:, pl.ds(pl.multiple_of(z * fz + k * fch, fch), fch)]
+
+    def down_src(z, k):
+        return w_down.at[pl.ds(pl.multiple_of(z * fz + k * fch, fch), fch), :]
+
+    def up_dst(d, k):
+        return up.at[tile(d, dr), pl.ds(k * fch, fch)]
+
+    def down_dst(d, k):
+        return down.at[pl.ds(k * fch, fch), tile(d, dr)]
+
+    kinds = ((up_src, up_dst), (down_src, down_dst))
+
+    def z_weights(k, which):
+        for j in which:
+            for kind, (src, dst) in enumerate(kinds):
+                cp.go(
+                    lambda: src(p.z_plus(j), k),
+                    lambda: dst(p.d, k),
+                    z_w.at[j - 1, k, kind],
+                    lambda: p.at_z(p.z_plus(j)),
+                )
+
+    def forward(k, j):
+        d_src = lax.rem(p.z - j + Z, Z) * Y + p.y
+        for kind, (_, dst) in enumerate(kinds):
+            landed(p, lambda: dst(d_src, k), z_w.at[j - 1, k, kind])
+            cp.go(lambda: dst(d_src, k), lambda: dst(d_src, k), y_w.at[j, k, kind], p.at_y)
+
+    def weights_here(k):
+        for j in range(Z):
+            d_src = lax.rem(p.z - j + Z, Z) * Y + 1 - p.y
+            for kind, (_, dst) in enumerate(kinds):
+                landed(p, lambda: dst(d_src, k), y_w.at[j, k, kind])
+
+    own_weights = []
+    for k in range(nch):
+        for kind, (src, dst) in enumerate(kinds):
+            cp.go(lambda: src(p.z, k), lambda: dst(p.d, k), y_w.at[0, k, kind], p.at_y)
+            copy = pltpu.make_async_copy(src(p.z, k), dst(p.d, k), loads.at[5 + 2 * k + kind])
+            copy.start()
+            own_weights.append(copy)
+
+    for copy in first:
+        copy.wait()
+    joined[pl.ds(0, n_text)] = jnp.where(drop[0] == 1, null_v[...], text_v[...])
+    shift, scale, gate = level[0:1, :], 1.0 + level[1:2, :], level[2:3, :]
+
+    def stats(at):
+        values = joined[at, :].astype(F32)
+        centred = values - jnp.mean(values, axis=-1, keepdims=True)
+        inv_std = lax.rsqrt(jnp.mean(centred * centred, axis=-1, keepdims=True) + EPS)
+        return values, centred * inv_std, inv_std
+
+    mine = pl.multiple_of(((p.c * Z + p.z) * X + p.x) * n, n)
+
+    def prepare(b):
+        at = pl.ds(pl.multiple_of(b * n_text, n_text), n_text)
+        to = pl.ds(pl.multiple_of(mine + b * n_text, n_text), n_text)
+        _, normed, _ = stats(at)
+        tok[0, to, :] = (normed * scale + shift).astype(BF16)
+        tok[1, to, :] = (d_out[at, :].astype(F32) * gate).astype(BF16)
+
+    each(0, n // n_text, prepare)
+
+    slots = [(0, p.z, None)]
+    for s in range(Z - 1):
+        slots.append((1 + 2 * s, p.z - 1 - s, p.z - 1 - s >= 0))
+        slots.append((2 + 2 * s, p.z + 1 + s, p.z + 1 + s < Z))
+
+    def block(sample, x, c):
+        return tok.at[:, at_rows(c, sample, x), :]
+
+    def spread(slot, sample, when):
+        def ref():
+            return block(sample, p.x, p.c)
+
+        for j in range(1, X):
+            cp.go(ref, ref, x_tok.at[j - 1, slot], lambda: p.at_x(p.x_plus(j)), when)
+        cp.go(ref, ref, c_tok.at[0, slot], p.at_c, when)
+
+    def pass_on(s, i):
+        for way in (1, -1):
+            sample = p.z - s * way
+            inside = (sample >= 0) & (p.z + 1 < Z) if way == 1 else (sample < Z) & (p.z >= 1)
+
+            def ref():
+                return tok.at[i, at_rows(p.c, sample, p.x), :]
+
+            cp.go(ref, ref, z_tok.at[(0 if way == 1 else 1), s, i], lambda: p.at_z(p.z + way), inside)
+
+    for i in range(2):
+        pass_on(0, i)
+    spread(*slots[0])
+    for s in range(Z - 1):
+        for i in range(2):
+            for side in (0, 1):
+                slot, sample, valid = slots[1 + 2 * s + side]
+                landed(p, lambda: tok.at[i, at_rows(p.c, sample, p.x), :], z_tok.at[side, s, i], valid)
+            if s < Z - 2:
+                pass_on(s + 1, i)
+        if s == min(1, Z - 2):
+            z_weights(0, far)
+        for side in (0, 1):
+            spread(*slots[1 + 2 * s + side])
+    z_weights(1, far)
+    for j in far:
+        forward(0, j)
+    for slot, sample, valid in slots:
+        for j in range(1, X):
+            x = lax.rem(p.x - j + X, X)
+
+            def ref():
+                return block(sample, x, p.c)
+
+            landed(p, ref, x_tok.at[j - 1, slot], valid)
+            cp.go(ref, ref, c_tok.at[j, slot], p.at_c, valid)
+    for k in range(2, nch):
+        z_weights(k, far)
+    for slot, sample, valid in slots:
+        for j in range(X):
+            x = lax.rem(p.x - j + X, X)
+            landed(p, lambda: block(sample, x, 1 - p.c), c_tok.at[j, slot], valid)
+
+    tall = 256
+
+    def hidden(k):
+        units = pl.ds(k * fch, fch)
+
+        def act(r):
+            at = pl.ds(pl.multiple_of(r * tall, tall), tall)
+            pre = dot(tok[0, at, :], up[:, units], ((1,), (0,)))
+            d_hid = dot(tok[1, at, :], down[units, :], ((1,), (1,)))
+            values, back = jax.vjp(gelu_tanh, pre)
+            hid[at, units] = values.astype(BF16)
+            d_pre[at, units] = back(d_hid)[0].astype(BF16)
+
+        each(0, rows // tall, act)
+
+    def y_copy(i, kind):
+        k, j, z = place_of(i)
+        ref = g_ref(kind, z, k)
+        return pltpu.make_async_remote_copy(
+            src_ref=ref((g_up, g_down)[kind]),
+            dst_ref=ref((y_up, y_down)[kind]),
+            send_sem=y_out.at[j, k, kind],
+            recv_sem=y_g.at[j, k, kind],
+            device_id=p.at_y(),
+            device_id_type=MESH,
+        )
+
+    def place_of(i):
+        k = i // Z
+        j = lax.rem(i - k * Z + Z // 2, Z)
+        return k, j, p.z_plus(j)
+
+    def units_of(k):
+        return pl.ds(pl.multiple_of(k * fch, fch), fch)
+
+    def g_ref(kind, z, k):
+        def ref(buffer):
+            return buffer.at[tile(z, dr), units_of(k)] if kind == 0 else buffer.at[units_of(k), tile(z, dr)]
+
+        return ref
+
+    def product(kind, z, y, k):
+        features = tile(z * Y + y, dr)
+        if kind == 0:
+            return dot(tok[0, :, features], d_pre[:, units_of(k)], ((0,), (0,)))
+        return dot(hid[:, units_of(k)], tok[1, :, features], ((0,), (0,)))
+
+    def peer_gradient(i):
+        k, j, z = place_of(i)
+        for kind in range(2):
+            g_ref(kind, z, k)((g_up, g_down)[kind])[...] = product(kind, z, 1 - p.y, k).astype(BF16)
+            y_copy(i, kind).start()
+
+    def out_ref(kind, z, k):
+        cols = pl.ds(pl.multiple_of(z * fz + k * fch, fch), fch)
+        return up_out.at[:, cols] if kind == 0 else down_out.at[cols, :]
+
+    def z_copy(i, kind):
+        k, j, z = place_of(i)
+        return pltpu.make_async_remote_copy(
+            src_ref=g_ref(kind, z, k)((y_up, y_down)[kind]),
+            dst_ref=out_ref(kind, p.z, k),
+            send_sem=z_out.at[j, k, kind],
+            recv_sem=z_g.at[j, k, kind],
+            device_id=p.at_z(z),
+            device_id_type=MESH,
+        )
+
+    def kept(i, kind):
+        k, j, z = place_of(i)
+        return pltpu.make_async_copy(
+            g_ref(kind, z, k)((y_up, y_down)[kind]), out_ref(kind, p.z, k), z_out.at[j, k, kind]
+        )
+
+    def own_gradient(i):
+        k, j, z = place_of(i)
+        for kind in range(2):
+            y_copy(i, kind).wait_recv()
+            ref = g_ref(kind, z, k)((y_up, y_down)[kind])
+            ref[...] = (product(kind, z, p.y, k) + ref[...].astype(F32)).astype(BF16)
+            pl.when(j > 0)(lambda: z_copy(i, kind).start())
+            pl.when(j == 0)(lambda: kept(i, kind).start())
+
+    count = nch * Z
+    started, ended = [0], [0]
+
+    def some_peer(number):
+        last = min(count, started[0] + number)
+        if last > started[0]:
+            each(started[0], last, peer_gradient)
+            started[0] = last
+
+    def some_own(number):
+        last = min(started[0], ended[0] + number)
+        if last > ended[0]:
+            each(ended[0], last, own_gradient)
+            ended[0] = last
+
+    for copy in own_weights:
+        copy.wait()
+    weights_here(0)
+    hidden(0)
+    for k in range(1, nch):
+        for at, j in enumerate(far):
+            forward(k, j)
+            if at == (1 if k == 1 else 0):
+                some_peer(1)
+        if k == nch - 1:
+            some_own(2)
+            some_peer(k * Z - started[0])
+        weights_here(k)
+        if k == nch - 1:
+            some_own(1)
+        hidden(k)
+
+    wide = 256
+
+    def summand(i, c, b):
+        at = pl.ds(pl.multiple_of(c * half, half), half)
+        cols = pl.ds(pl.multiple_of(b * wide, wide), wide)
+        if i == 0:
+            return cols, dot(hid[at, :], down[:, cols], ((1,), (0,)))
+        return cols, dot(d_pre[at, :], up[cols, :], ((1,), (1,)))
+
+    order = []
+    for i in range((Z + 1) // 2):
+        order += [Z - 1 - i] + ([i] if i != Z - 1 - i else [])
+
+    def sample_rows(t):
+        return pl.ds(t * X * n, X * n)
+
+    def c_copy(i, t):
+        return pltpu.make_async_remote_copy(
+            src_ref=s_buf.at[i, sample_rows(t), :],
+            dst_ref=c_buf.at[i, sample_rows(t), :],
+            send_sem=c_s.at[0, i, t],
+            recv_sem=c_s.at[1, i, t],
+            device_id=p.at_c(),
+            device_id_type=MESH,
+        )
+
+    def x_rows(t, x):
+        return pl.ds(pl.multiple_of((t * X + x) * n, n), n)
+
+    def own_rows(t):
+        return x_rows(t, p.x)
+
+    for i in range(2):
+
+        def other(b):
+            cols, value = summand(i, 1 - p.c, b)
+            s_buf[i, :, cols] = value.astype(BF16)
+
+        each(0, width // wide, other)
+        for t in order:
+            c_copy(i, t).start()
+        some_own(1)
+        for t in order:
+            c_copy(i, t).wait_recv()
+
+        def mine_too(b):
+            cols, value = summand(i, p.c, b)
+            c_buf[i, :, cols] = (value + c_buf[i, :, cols].astype(F32)).astype(BF16)
+
+        each(0, width // wide, mine_too)
+        for t in order:
+            for j in range(1, X):
+                x = p.x_plus(j)
+                cp.go(
+                    lambda: c_buf.at[i, x_rows(t, x), :],
+                    lambda: x_buf.at[j - 1, i, t],
+                    x_s.at[j - 1, i, t],
+                    lambda: p.at_x(x),
+                )
+        some_own(1)
+        some_peer(2)
+    some_peer(count)
+
+    def x_stage(t, i):
+        for j in range(X - 1):
+            landed(p, lambda: x_buf.at[j, i, t], x_s.at[j, i, t])
+            add_into(c_buf.at[i, own_rows(t), :], x_buf.at[j, i, t], n, 16)
+
+    def chain(t, i, hop):
+        for way, here_z, slot, sem in (
+            (1, hop, t, r_s),
+            (-1, Z - 1 - hop, t, l_s),
+        ):
+            if (t - here_z) * way <= 0:
+                continue
+            here = p.z == here_z
+            target = Z if way == -1 and here_z - 1 == t else t
+            if hop == 0:
+                source = lambda: c_buf.at[i, own_rows(t), :]
+            else:
+                source = lambda: l_buf.at[i, t]
+                landed(p, source, sem.at[i, t], here)
+                pl.when(here)(lambda: add_into(l_buf.at[i, t], c_buf.at[i, own_rows(t), :], n, 16))
+            cp.go(source, lambda: l_buf.at[i, target], sem.at[i, t], lambda: p.at_z(here_z + way), here)
+
+    is_dropped = (drop[0] == 1).astype(F32)
+
+    def arrived(i):
+        for t in range(Z):
+            here = p.z == t
+            if t > 0:
+                landed(p, lambda: l_buf.at[i, t], r_s.at[i, t], here)
+            if t < Z - 1:
+                landed(p, lambda: l_buf.at[i, Z], l_s.at[i, t], here)
+
+    def total(i, b, at):
+        mine_at = pl.ds(pl.multiple_of((p.z * X + p.x) * n + b * n_text, n_text), n_text)
+        own = c_buf[i, mine_at, :].astype(F32)
+        low = l_buf[i, p.z, at, :].astype(F32)
+        high = l_buf[i, Z, at, :].astype(F32)
+        return own + jnp.where(p.z > 0, low, 0.0) + jnp.where(p.z < Z - 1, high, 0.0)
+
+    def output(b):
+        at = pl.ds(pl.multiple_of(b * n_text, n_text), n_text)
+        fin[0, at, :] = (joined[at, :].astype(F32) + gate * total(0, b, at)).astype(BF16)
+
+    def input_gradient(b):
+        at = pl.ds(pl.multiple_of(b * n_text, n_text), n_text)
+        _, normed, inv_std = stats(at)
+        d_normed = total(1, b, at) * scale
+        d_full = d_out[at, :].astype(F32) + inv_std * (
+            d_normed
+            - jnp.mean(d_normed, axis=-1, keepdims=True)
+            - normed * jnp.mean(d_normed * normed, axis=-1, keepdims=True)
+        )
+        fin[1, at, :] = d_full.astype(BF16)
+
+        @pl.when(b == 0)
+        def _():
+            null[0] = (d_full * is_dropped).astype(BF16)
+
+    def share(src, out, x_sem, c_sem):
+        for j in range(1, X):
+            cp.go(src, lambda: out(p.m), x_sem.at[j - 1], lambda: p.at_x(p.x_plus(j)))
+        cp.go(src, lambda: out(p.m), c_sem.at[0], p.at_c)
+        cp.local(src, lambda: out(p.m))
+
+    def relay(out, x_sem, c_sem):
+        for j in range(1, X):
+            quarter = lax.rem(p.x - j + X, X) * C + p.c
+            landed(p, lambda: out(quarter), x_sem.at[j - 1])
+            cp.go(lambda: out(quarter), lambda: out(quarter), c_sem.at[j], p.at_c)
+
+    def settle(out, c_sem):
+        for j in range(X):
+            quarter = lax.rem(p.x - j + X, X) * C + 1 - p.c
+            landed(p, lambda: out(quarter), c_sem.at[j])
+
+    outs = [lambda quarter: out_all.at[quarter], lambda quarter: d_tok_all.at[quarter]]
+
+    def null_out(quarter):
+        return null_all.at[quarter]
+
+    sums = [(t, i) for i in range(2) for t in order]
+    lag = 2
+    steps = len(sums) + lag * (Z - 2)
+    for step in range(steps):
+        if step % 2 == 0:
+            some_own(1)
+        if step < len(sums):
+            x_stage(*sums[step])
+        for hop in range(Z - 1):
+            at = step - hop * lag
+            if 0 <= at < len(sums):
+                chain(*sums[at], hop)
+        if step == Z + lag * (Z - 2) + 1:
+            arrived(0)
+            each(0, n // n_text, output)
+            share(lambda: fin.at[0], outs[0], f_x.at[0], f_c.at[0])
+    arrived(1)
+    each(0, n // n_text, input_gradient)
+
+    cp.go(lambda: null.at[0], lambda: null_y.at[...], n_y.at[0], p.at_y)
+    share(lambda: fin.at[1], outs[1], f_x.at[1], f_c.at[1])
+    relay(outs[0], f_x.at[0], f_c.at[0])
+    landed(p, lambda: null_y.at[...], n_y.at[0])
+    null[1] = (null[0].astype(F32) + null_y[...].astype(F32)).astype(BF16)
+    for j in range(1, Z):
+        cp.go(lambda: null.at[1], lambda: null_z.at[j - 1], n_z.at[j - 1], lambda: p.at_z(p.z_plus(j)))
+    some_peer(count)
+    some_own(count)
+    relay(outs[1], f_x.at[1], f_c.at[1])
+    for j in range(1, Z):
+        landed(p, lambda: null_z.at[j - 1], n_z.at[j - 1])
+    whole_null = null[1].astype(F32)
+    for j in range(1, Z):
+        whole_null = whole_null + null_z[j - 1].astype(F32)
+    null[2] = whole_null.astype(BF16)
+    share(lambda: null.at[2], null_out, n_x, n_c)
+    relay(null_out, n_x, n_c)
+    for i in range(2):
+        settle(outs[i], f_c.at[i])
+    settle(null_out, n_c)
+
+    def settled(i):
+        k, j, z = place_of(i)
+        for kind in range(2):
+            y_copy(i, kind).wait_send()
+
+            @pl.when(j > 0)
+            def _():
+                source = lax.rem(p.z - j + Z, Z)
+                landed(p, lambda: out_ref(kind, source, k), z_g.at[j, k, kind])
+                z_copy(i, kind).wait_send()
+
+            pl.when(j == 0)(lambda: kept(i, kind).wait())
+
+    each(0, count, settled)
+    for i in range(2):
+        for t in range(Z):
+            c_copy(i, t).wait_send()
+    cp.finish()
+
+
+def shards(
+    dp,
+    mp,
+    image_tokens,
+    text_tokens,
+    null_prompt,
+    drop_flags,
+    time_index,
+    modulation,
+    w_up,
+    w_down,
+    d_output,
+):
+    Z, X = dp // Y, mp // C
+    d_rows, ff_m = w_up.shape
+    fz = ff_m // Z
+    nch = fz // 256
+    width = d_rows * dp
+    n_text = text_tokens.shape[1] // mp
+    n = n_text + image_tokens.shape[1] // mp
+    rows = Z * mp * n
+    level = lax.dynamic_index_in_dim(modulation, time_index[0], 0, keepdims=False)
+
+    anywhere = pl.BlockSpec(memory_space=pl.ANY)
+    dma = pltpu.SemaphoreType.DMA
+    slots = 1 + 2 * (Z - 1)
+    sends = (
+        2 * nch * Z
+        + slots * (2 * X - 1)
+        + 4 * (Z - 1)
+        + 2 * nch * Z
+        + 2 * Z * (X - 1)
+        + 2 * 2 * Z * (Z - 1)
+        + 1
+        + (Z - 1)
+        + 3 * (X + 1)
+        + 3 * (X - 1)
+    )
+    every_out, every_d_tok, every_null, up_out, down_out = pl.pallas_call(
+        functools.partial(block_kernel, dp, mp, nch),
+        out_shape=(
+            jax.ShapeDtypeStruct((mp, n, width), BF16),
+            jax.ShapeDtypeStruct((mp, n, width), BF16),
+            jax.ShapeDtypeStruct((mp, n_text, width), BF16),
+            jax.ShapeDtypeStruct((d_rows, ff_m), BF16),
+            jax.ShapeDtypeStruct((ff_m, d_rows), BF16),
+        ),
+        in_specs=[
+            pl.BlockSpec(memory_space=pltpu.SMEM),
+            pl.BlockSpec(memory_space=pltpu.VMEM),
+        ]
+        + [anywhere] * 6,
+        out_specs=(anywhere,) * 5,
+        scratch_shapes=[
+            pltpu.VMEM((n, width), BF16),
+            pltpu.VMEM((n_text, width), BF16),
+            pltpu.VMEM((n_text, width), BF16),
+            pltpu.VMEM((n, width), BF16),
+            pltpu.VMEM((2, rows, width), BF16),
+            pltpu.VMEM((width, fz), BF16),
+            pltpu.VMEM((fz, width), BF16),
+            pltpu.VMEM((rows, fz), BF16),
+            pltpu.VMEM((rows, fz), BF16),
+            pltpu.VMEM((Z * d_rows, fz), BF16),
+            pltpu.VMEM((fz, Z * d_rows), BF16),
+            pltpu.VMEM((Z * d_rows, fz), BF16),
+            pltpu.VMEM((fz, Z * d_rows), BF16),
+            pltpu.VMEM((2, rows // C, width), BF16),
+            pltpu.VMEM((2, rows // C, width), BF16),
+            pltpu.VMEM((X - 1, 2, Z, n, width), BF16),
+            pltpu.VMEM((2, Z + 1, n, width), BF16),
+            pltpu.VMEM((2, n, width), BF16),
+            pltpu.VMEM((3, n_text, width), BF16),
+            pltpu.VMEM((n_text, width), BF16),
+            pltpu.VMEM((Z - 1, n_text, width), BF16),
+            dma((sends,)),
+            dma((2, Z - 1, 2)),
+            dma((X - 1, slots)),
+            dma((X, slots)),
+            dma((Z - 1, nch, 2)),
+            dma((Z, nch, 2)),
+            dma((Z, nch, 2)),
+            dma((Z, nch, 2)),
+            dma((Z, nch, 2)),
+            dma((Z, nch, 2)),
+            dma((2, 2, Z)),
+            dma((X - 1, 2, Z)),
+            dma((2, Z)),
+            dma((2, Z)),
+            dma((2, X - 1)),
+            dma((2, X)),
+            dma((1,)),
+            dma((Z - 1,)),
+            dma((X - 1,)),
+            dma((X,)),
+            dma((5 + 2 * nch,)),
+        ],
+        compiler_params=pltpu.CompilerParams(
+            collective_id=0, has_side_effects=True, vmem_limit_bytes=67043328
+        ),
+    )(drop_flags, level, image_tokens, text_tokens, null_prompt, d_output, w_up, w_down)
+
+    def whole(every):
+        text = every[:, :n_text].reshape(-1, width)
+        image = every[:, n_text:].reshape(-1, width)
+        return jnp.concatenate([text, image], axis=0)[None]
+
+    return (
+        whole(every_out),
+        whole(every_d_tok),
+        up_out.astype(F32),
+        down_out.astype(F32),
+        every_null.reshape(-1, width).astype(F32),
+    )
+
+
+def fits(dp, mp, image_tokens, text_tokens, w_up):
+    d_rows, ff_m = w_up.shape
+    return (
+        dp % Y == 0
+        and dp // Y > 1
+        and mp % C == 0
+        and mp // C > 1
+        and d_rows % 128 == 0
+        and ff_m % (dp // Y * 256) == 0
+        and ff_m > dp // Y * 256
+        and text_tokens.shape[1] % (mp * 16) == 0
+        and image_tokens.shape[1] % text_tokens.shape[1] == 0
+    )
+
+
+def program(dp, mp, image_tokens, text_tokens, null_prompt, drop_flags, time_index, modulation, w_up, w_down, d_output):
+    path = shards if fits(dp, mp, image_tokens, text_tokens, w_up) else generic
+    return path(
+        dp, mp, image_tokens, text_tokens, null_prompt, drop_flags, time_index, modulation, w_up, w_down, d_output
+    )
+
+
 def solution(mesh):
     placed = (
         P("dp", None, None),
@@ -182,7 +991,7 @@
         P("dp", None, None),
     )
     return jax.shard_map(
-        functools.partial(shards, mesh.shape["dp"], mesh.shape["mp"]),
+        functools.partial(program, mesh.shape["dp"], mesh.shape["mp"]),
         mesh=mesh,
         in_specs=placed,
         out_specs=(P("dp", None, None), P("dp", None, None), P("dp", "mp"), P("mp", "dp"), P()),

time: 638 us -> 359 us (0.56); the launches traced: 626 us -> 357 us
  waiting for transfers between devices: 378 us -> 0 us
  Pallas kernels: 0 us -> 341 us
  matrix products: 73.8 us -> 0 us
  starting transfers between devices: 50.5 us -> 0 us
  local copies, waits for them, and re-layouts: 49 us -> 5.45 us
  other arithmetic: 49.7 us -> 8.07 us
  between operations: 16.1 us -> 1.99 us
  blocking collectives: 9.2 us -> 0 us
    pallas_call x0 -> x1, Pallas kernels: none -> 341 us  [shards(): pl.pallas_call(functools.partial(block_kernel, dp, mp, nch), out_shape=(j...]
    ppermute x12 -> x0, waiting for transfers between devices: 157 us -> none  [swap(): return lax.ppermute(values, axis, [(i, i ^ bit) for i in range(size)])]
    all_gather x4 -> x0, waiting for transfers between devices: 135 us -> none  [the longest x2 102 us: gather(): lax.all_gather(rows, 'dp', axis=0, tiled=True, axis_index_groups=lines)]
    dot_general x16 -> x0, matrix products: 73.8 us -> none  [dot(): lax.dot_general(left, right, (dims, ((), ())), preferred_element_type=F32)]
    all_to_all x6 -> x0, waiting for transfers between devices: 60.1 us -> none  [the longest x1 44.5 us: shards(): lax.all_to_all(g_down.astype(BF16).reshape(f, dp, d_rows).transpose(1, 0,...]
    all_to_all x6 -> x0, starting transfers between devices: 38.2 us -> none  [the longest x2 13.3 us: scatter(): lax.all_to_all(total.astype(BF16).reshape(per_line, -1, width), 'dp', 0,...]
    psum x1 -> x0, waiting for transfers between devices: 24.6 us -> none  [shards(): null_sum = lax.psum(null_part, 'dp')]
    unnamed x69 -> x9, local copies, waits for them, and re-layouts: 17.3 us -> 1.85 us
  transfers between devices with their start and end apart: 23 -> 0, of which waited for: 16 -> 0; matrix products, arithmetic and copies ran while one was open for 24% -> 0% of each run, Pallas kernels for 0% -> 0%
where the time goes in v2:
time: 359 us; the launch traced here: 357 us
  Pallas kernels  341 us (95%)
  other arithmetic  8.07 us (2%)
  local copies, waits for them, and re-layouts  5.45 us (2%)
    pallas_call x1, Pallas kernels, shards(): pl.pallas_call(functools.partial(block_kernel, dp, mp, nch), out_shape=(j...  341 us

profile of v2, /device:TPU:9, one launch (start us, length us, event | category | flops | bytes accessed | tf_op | source)
XLA Modules:
  0.0 356.9 jit_solution(11403081816920230071)
XLA Ops:
  1.3 1.0 constant_dynamic-slice_fusion
  2.3 0.6 copy.16
  3.6 341.4 %shard_map.128 = (bf16[4,64,3072]{2,1,0:T(8,128)(2,1)}, bf16[4,64,3072]{2,1,0:T(8,128)(2,1)}, bf16[4,16,3072]{2,1,0:T(8,128)(2,1)}, bf16[384,3072]{1,0:T(8,128)(2,1)}, bf16[3072,384]{1,0:T(8,128)(2,1)}) custom-call(s32[1]{0:T(128)S(6)} %copy.17.drop, f32[3,3072]{1,0:T(4,128)} %bitcast.22, bf16[1,192,3072]{2,1,0:T(8,128)(2,1)} %image.1, ...), custom_call_target="tpu_custom_call" | custom-call | tf_op jit(solution)/shard_map/pallas_call | solution.py:881
  345.0 0.0 copy-start.2
  345.0 1.5 slice.13
  346.5 0.3 copy-done.2
  346.8 0.1 slice.15
  346.9 1.0 slice.12
  347.9 0.0 copy-start.1
  347.9 1.9 maximum_bitcast_fusion
  349.8 0.9 copy-done.1
  350.7 0.0 copy-start
  350.7 2.8 convert_element_type.12
  353.5 0.0 copy-done
  353.5 0.0 copy-start.3
  353.5 2.5 convert_element_type.13
  356.0 0.0 copy-done.3
  356.0 1.0 bitcast_convert_fusion
  (1 shorter events, 0.0 us)
Async XLA Ops:
  345.0 1.8 copy-start.2
  347.9 2.8 copy-start.1
  350.7 2.8 copy-start
  353.5 2.5 copy-start.3

commit v3 on v2

--- a/solution.py
+++ b/solution.py
@@ -376,7 +376,11 @@
     half = Z * X * n
     rows = C * half
     cp = Copies(send)
-    far = [2, 1, 3] if Z == 4 else list(range(1, Z))
+    if Z == 4:
+        one = jnp.where(p.z < 2, 1, 3)
+        hops = [2, one, Z - one]
+    else:
+        hops = list(range(1, Z))
 
     def at_rows(c, z, x):
         return pl.ds(pl.multiple_of(((c * Z + z) * X + x) * n, n), n)
@@ -498,12 +502,14 @@
                 landed(p, lambda: tok.at[i, at_rows(p.c, sample, p.x), :], z_tok.at[side, s, i], valid)
             if s < Z - 2:
                 pass_on(s + 1, i)
-        if s == min(1, Z - 2):
-            z_weights(0, far)
         for side in (0, 1):
             spread(*slots[1 + 2 * s + side])
-    z_weights(1, far)
-    for j in far:
+        if s == min(1, Z - 2):
+            z_weights(0, hops)
+            forward(0, hops[0])
+    forward(0, hops[1])
+    z_weights(1, hops)
+    for j in hops[2:]:
         forward(0, j)
     for slot, sample, valid in slots:
         for j in range(1, X):
@@ -515,7 +521,7 @@
             landed(p, ref, x_tok.at[j - 1, slot], valid)
             cp.go(ref, ref, c_tok.at[j, slot], p.at_c, valid)
     for k in range(2, nch):
-        z_weights(k, far)
+        z_weights(k, hops)
     for slot, sample, valid in slots:
         for j in range(X):
             x = lax.rem(p.x - j + X, X)
@@ -548,13 +554,17 @@
             device_id_type=MESH,
         )
 
+    along = sorted(range(1, Z), key=lambda j: -min(j, Z - j))
+    pieces = [(k, j) for j in along for k in range(nch - 1)]
+    early = len(pieces)
+    pieces += [(nch - 1, j) for j in along] + [(k, 0) for k in range(nch)]
+
     def place_of(i):
-        k = i // Z
-        j = lax.rem(i - k * Z + Z // 2, Z)
+        k, j = pieces[i]
         return k, j, p.z_plus(j)
 
     def units_of(k):
-        return pl.ds(pl.multiple_of(k * fch, fch), fch)
+        return pl.ds(k * fch, fch)
 
     def g_ref(kind, z, k):
         def ref(buffer):
@@ -601,8 +611,10 @@
             y_copy(i, kind).wait_recv()
             ref = g_ref(kind, z, k)((y_up, y_down)[kind])
             ref[...] = (product(kind, z, p.y, k) + ref[...].astype(F32)).astype(BF16)
-            pl.when(j > 0)(lambda: z_copy(i, kind).start())
-            pl.when(j == 0)(lambda: kept(i, kind).start())
+            if j > 0:
+                z_copy(i, kind).start()
+            else:
+                kept(i, kind).start()
 
     count = nch * Z
     started, ended = [0], [0]
@@ -610,31 +622,36 @@
     def some_peer(number):
         last = min(count, started[0] + number)
         if last > started[0]:
-            each(started[0], last, peer_gradient)
+            for i in range(started[0], last):
+                peer_gradient(i)
             started[0] = last
 
     def some_own(number):
         last = min(started[0], ended[0] + number)
         if last > ended[0]:
-            each(ended[0], last, own_gradient)
+            for i in range(ended[0], last):
+                own_gradient(i)
             ended[0] = last
 
     for copy in own_weights:
         copy.wait()
     weights_here(0)
     hidden(0)
+    for j in hops:
+        forward(1, j)
+        if j is hops[1]:
+            some_peer(1)
     for k in range(1, nch):
-        for at, j in enumerate(far):
-            forward(k, j)
-            if at == (1 if k == 1 else 0):
-                some_peer(1)
-        if k == nch - 1:
-            some_own(2)
-            some_peer(k * Z - started[0])
+        if k + 1 < nch:
+            for j in hops[:-1]:
+                forward(k + 1, j)
         weights_here(k)
-        if k == nch - 1:
+        hidden(k)
+        if k + 1 < nch:
+            forward(k + 1, hops[-1])
+        if k == nch - 2:
             some_own(1)
-        hidden(k)
+            some_peer(early - started[0])
 
     wide = 256
 
@@ -668,8 +685,7 @@
     def own_rows(t):
         return x_rows(t, p.x)
 
-    for i in range(2):
-
+    def other_core(i):
         def other(b):
             cols, value = summand(i, 1 - p.c, b)
             s_buf[i, :, cols] = value.astype(BF16)
@@ -677,7 +693,8 @@
         each(0, width // wide, other)
         for t in order:
             c_copy(i, t).start()
-        some_own(1)
+
+    def own_core(i):
         for t in order:
             c_copy(i, t).wait_recv()
 
@@ -695,9 +712,6 @@
                     x_s.at[j - 1, i, t],
                     lambda: p.at_x(x),
                 )
-        some_own(1)
-        some_peer(2)
-    some_peer(count)
 
     def x_stage(t, i):
         for j in range(X - 1):
@@ -774,40 +788,71 @@
             quarter = lax.rem(p.x - j + X, X) * C + 1 - p.c
             landed(p, lambda: out(quarter), c_sem.at[j])
 
-    outs = [lambda quarter: out_all.at[quarter], lambda quarter: d_tok_all.at[quarter]]
+    def part(i, s):
+        def out(quarter):
+            if s == 0:
+                at = pl.ds(pl.multiple_of(quarter * n_text, n_text), n_text)
+            else:
+                at = pl.ds(pl.multiple_of(every_text + quarter * n_image, n_text), n_image)
+            return (out_all, d_tok_all)[i].at[at, :]
+
+        return out
+
+    def share_tokens(i):
+        for s, at in enumerate((pl.ds(0, n_text), pl.ds(n_text, n_image))):
+            share(lambda: fin.at[i, at, :], part(i, s), f_x.at[2 * i + s], f_c.at[2 * i + s])
+
+    def relay_tokens(i):
+        for s in range(2):
+            relay(part(i, s), f_x.at[2 * i + s], f_c.at[2 * i + s])
 
     def null_out(quarter):
         return null_all.at[quarter]
 
-    sums = [(t, i) for i in range(2) for t in order]
-    lag = 2
+    sums = [(t, i) for i in (1, 0) for t in order]
+    lag = 3
     steps = len(sums) + lag * (Z - 2)
-    for step in range(steps):
-        if step % 2 == 0:
-            some_own(1)
+
+    def take(step):
         if step < len(sums):
             x_stage(*sums[step])
-        for hop in range(Z - 1):
+            chain(*sums[step], 0)
+        if step < 3 or step in (len(sums) - 2, len(sums) + 1):
+            some_own(1)
+        for hop in range(Z - 2, 0, -1):
             at = step - hop * lag
             if 0 <= at < len(sums):
                 chain(*sums[at], hop)
         if step == Z + lag * (Z - 2) + 1:
-            arrived(0)
-            each(0, n // n_text, output)
-            share(lambda: fin.at[0], outs[0], f_x.at[0], f_c.at[0])
-    arrived(1)
-    each(0, n // n_text, input_gradient)
-
-    cp.go(lambda: null.at[0], lambda: null_y.at[...], n_y.at[0], p.at_y)
-    share(lambda: fin.at[1], outs[1], f_x.at[1], f_c.at[1])
-    relay(outs[0], f_x.at[0], f_c.at[0])
-    landed(p, lambda: null_y.at[...], n_y.at[0])
-    null[1] = (null[0].astype(F32) + null_y[...].astype(F32)).astype(BF16)
-    for j in range(1, Z):
-        cp.go(lambda: null.at[1], lambda: null_z.at[j - 1], n_z.at[j - 1], lambda: p.at_z(p.z_plus(j)))
+            arrived(1)
+            each(0, n // n_text, input_gradient)
+            cp.go(lambda: null.at[0], lambda: null_y.at[...], n_y.at[0], p.at_y)
+            share_tokens(1)
+            some_own(count)
+            landed(p, lambda: null_y.at[...], n_y.at[0])
+            null[1] = (null[0].astype(F32) + null_y[...].astype(F32)).astype(BF16)
+            for j in range(1, Z):
+                cp.go(lambda: null.at[1], lambda: null_z.at[j - 1], n_z.at[j - 1], lambda: p.at_z(p.z_plus(j)))
+
+    some_own(1)
+    some_peer(1)
+    other_core(1)
+    some_own(1)
+    own_core(1)
+    some_own(1)
+    some_peer(2)
+    other_core(0)
+    take(0)
+    own_core(0)
+    some_peer(count)
+    for step in range(1, steps):
+        take(step)
     some_peer(count)
     some_own(count)
-    relay(outs[1], f_x.at[1], f_c.at[1])
+    relay_tokens(1)
+    arrived(0)
+    each(0, n // n_text, output)
+    share_tokens(0)
     for j in range(1, Z):
         landed(p, lambda: null_z.at[j - 1], n_z.at[j - 1])
     whole_null = null[1].astype(F32)
@@ -815,25 +860,26 @@
         whole_null = whole_null + null_z[j - 1].astype(F32)
     null[2] = whole_null.astype(BF16)
     share(lambda: null.at[2], null_out, n_x, n_c)
+    relay_tokens(0)
     relay(null_out, n_x, n_c)
     for i in range(2):
-        settle(outs[i], f_c.at[i])
+        for s in range(2):
+            settle(part(i, s), f_c.at[2 * i + s])
     settle(null_out, n_c)
 
     def settled(i):
         k, j, z = place_of(i)
         for kind in range(2):
             y_copy(i, kind).wait_send()
-
-            @pl.when(j > 0)
-            def _():
+            if j > 0:
                 source = lax.rem(p.z - j + Z, Z)
                 landed(p, lambda: out_ref(kind, source, k), z_g.at[j, k, kind])
                 z_copy(i, kind).wait_send()
-
-            pl.when(j == 0)(lambda: kept(i, kind).wait())
-
-    each(0, count, settled)
+            else:
+                kept(i, kind).wait()
+
+    for i in range(count):
+        settled(i)
     for i in range(2):
         for t in range(Z):
             c_copy(i, t).wait_send()
@@ -875,14 +921,14 @@
         + 2 * 2 * Z * (Z - 1)
         + 1
         + (Z - 1)
-        + 3 * (X + 1)
-        + 3 * (X - 1)
+        + 5 * (X + 1)
+        + 5 * (X - 1)
     )
     every_out, every_d_tok, every_null, up_out, down_out = pl.pallas_call(
         functools.partial(block_kernel, dp, mp, nch),
         out_shape=(
-            jax.ShapeDtypeStruct((mp, n, width), BF16),
-            jax.ShapeDtypeStruct((mp, n, width), BF16),
+            jax.ShapeDtypeStruct((mp * n, width), BF16),
+            jax.ShapeDtypeStruct((mp * n, width), BF16),
             jax.ShapeDtypeStruct((mp, n_text, width), BF16),
             jax.ShapeDtypeStruct((d_rows, ff_m), BF16),
             jax.ShapeDtypeStruct((ff_m, d_rows), BF16),
@@ -929,8 +975,8 @@
             dma((X - 1, 2, Z)),
             dma((2, Z)),
             dma((2, Z)),
-            dma((2, X - 1)),
-            dma((2, X)),
+            dma((4, X - 1)),
+            dma((4, X)),
             dma((1,)),
             dma((Z - 1,)),
             dma((X - 1,)),
@@ -942,14 +988,9 @@
         ),
     )(drop_flags, level, image_tokens, text_tokens, null_prompt, d_output, w_up, w_down)
 
-    def whole(every):
-        text = every[:, :n_text].reshape(-1, width)
-        image = every[:, n_text:].reshape(-1, width)
-        return jnp.concatenate([text, image], axis=0)[None]
-
     return (
-        whole(every_out),
-        whole(every_d_tok),
+        every_out[None],
+        every_d_tok[None],
         up_out.astype(F32),
         down_out.astype(F32),
         every_null.reshape(-1, width).astype(F32),
@@ -960,7 +1001,7 @@
     d_rows, ff_m = w_up.shape
     return (
         dp % Y == 0
-        and dp // Y > 1
+        and dp // Y > 2
         and mp % C == 0
         and mp // C > 1
         and d_rows % 128 == 0

time: 359 us -> 328 us (0.914)
  Pallas kernels: 341 us -> 313 us
    pallas_call x1, Pallas kernels: 341 us -> 313 us  [shards(): pl.pallas_call(functools.partial(block_kernel, dp, mp, nch), out_shape=(j...]
where the time goes in v3:
time: 328 us
  Pallas kernels  313 us (95%)
  other arithmetic  8.02 us (2%)
  local copies, waits for them, and re-layouts  4.76 us (1%)
    pallas_call x1, Pallas kernels, shards(): pl.pallas_call(functools.partial(block_kernel, dp, mp, nch), out_shape=(j...  313 us

profile of v3, /device:TPU:9, one launch (start us, length us, event | category | flops | bytes accessed | tf_op | source)
XLA Modules:
  0.0 328.1 jit_solution(9461567722269142333)
XLA Ops:
  1.3 1.0 constant_dynamic-slice_fusion
  2.3 0.6 copy.16
  3.6 313.4 %shard_map.128 = (bf16[256,3072]{1,0:T(8,128)(2,1)}, bf16[256,3072]{1,0:T(8,128)(2,1)}, bf16[4,16,3072]{2,1,0:T(8,128)(2,1)}, bf16[384,3072]{1,0:T(8,128)(2,1)}, bf16[3072,384]{1,0:T(8,128)(2,1)}) custom-call(s32[1]{0:T(128)S(6)} %copy.19.drop, f32[3,3072]{1,0:T(4,128)} %bitcast.14, bf16[1,192,3072]{2,1,0:T(8,128)(2,1)} %image.1, bf16[1,64,3072]{2,1,0:T(8,128)(2,1)} %text.1, ...), custom_call_target="tpu_custom_call" | custom-call | tf_op jit(solution)/shard_map/pallas_call | solution.py:927
  317.0 0.0 copy-start
  317.0 4.6 %convert_element_type.12 = f32[384,3072]{1,0:T(8,128)} convert(bf16[384,3072]{1,0:T(8,128)(2,1)} %get-tuple-element.12) | non-fusion elementwise | flops 1179648 | bytes 7077888 | tf_op jit(solution)/shard_map/convert_element_type | solution.py:994
  321.5 0.0 copy-done
  321.5 0.0 copy-start.3
  321.5 0.0 copy-start.2
  321.5 2.5 convert_element_type.13
  324.0 0.0 copy-done.3
  324.0 1.0 bitcast_convert_fusion
  325.0 0.0 copy-done.2
  325.0 0.0 copy-start.1
  325.0 1.1 copy.21
  326.1 0.8 copy-done.1
  327.0 1.1 copy.22
Async XLA Ops:
  317.0 4.6 %copy-start = (bf16[3072,384]{1,0:T(8,128)(2,1)S(1)}, bf16[3072,384]{1,0:T(8,128)(2,1)}, u32[]{:S(2)}) copy-start(bf16[3072,384]{1,0:T(8,128)(2,1)} %get-tuple-element.13) | copy-start | bytes 7077892
  321.5 2.5 copy-start.3
  321.5 3.5 %copy-start.2 = (bf16[256,3072]{1,0:T(8,128)(2,1)S(1)}, bf16[256,3072]{1,0:T(8,128)(2,1)}, u32[]{:S(2)}) copy-start(bf16[256,3072]{1,0:T(8,128)(2,1)} %get-tuple-element.10) | copy-start | bytes 4718596
  325.0 2.0 copy-start.1
